TPU v7x, 32 devices: a whole 2x2x4 slice. The times are simulated.
32 devices in a mesh: rep: 1, dp: 32 (over x, y, z, core).
Axes of the slice: x: 2, y: 2, z: 4, core: 2. Of those that a mesh axis runs over, the one named last changes fastest.
Arguments:
- x: bfloat16 [32, 2048, 1024], P(('rep', 'dp'))
- dy: bfloat16 [32, 2048, 1024], P(('rep', 'dp'))
- w_gate: bfloat16 [2, 1024, 2816], replicated
- w_up: bfloat16 [2, 1024, 2816], replicated
- w_down: bfloat16 [2, 2816, 1024], replicated
- m_w_gate: float32 [2, 1024, 2816], P(None, 'dp')
- m_w_up: float32 [2, 1024, 2816], P(None, 'dp')
- m_w_down: float32 [2, 2816, 1024], P(None, 'dp')
- v_w_gate: float32 [2, 1024, 2816], P(None, 'dp')
- v_w_up: float32 [2, 1024, 2816], P(None, 'dp')
- v_w_down: float32 [2, 2816, 1024], P(None, 'dp')
Outputs:
- output 1: bfloat16 [2, 1024, 2816], P('rep')
- output 2: bfloat16 [2, 1024, 2816], P('rep')
- output 3: bfloat16 [2, 2816, 1024], P('rep')
- output 4: float32 [2, 1024, 2816], P('rep', 'dp')
- output 5: float32 [2, 1024, 2816], P('rep', 'dp')
- output 6: float32 [2, 2816, 1024], P('rep', 'dp')
- output 7: float32 [2, 1024, 2816], P('rep', 'dp')
- output 8: float32 [2, 1024, 2816], P('rep', 'dp')
- output 9: float32 [2, 2816, 1024], P('rep', 'dp')
All inputs are finite; a program needn't handle non-finite values.
Results may differ from a plain program's by a relative error of at most 0.02.
Values are sent between devices in bfloat16 or wider.
A program may use at most 2 GiB of HBM per device.

v0:
```python
import jax
import jax.numpy as jnp
from jax import lax

NAMES = ("w_gate", "w_up", "w_down")


def matmul(a, w):
    return jnp.dot(a, w, preferred_element_type=jnp.float32).astype(jnp.bfloat16)


def normed(h):
    wide = h.astype(jnp.float32)
    scale = lax.rsqrt(jnp.mean(wide**2, -1, keepdims=True) + 1e-6)
    return (wide * scale).astype(jnp.bfloat16)


def layer(h, w):
    a = normed(h)
    gate = jnp.dot(a, w["w_gate"], preferred_element_type=jnp.float32)
    up = jnp.dot(a, w["w_up"], preferred_element_type=jnp.float32)
    return h + matmul((jax.nn.silu(gate) * up).astype(jnp.bfloat16), w["w_down"])


def adamw(w, m, v, g):
    m = 0.9 * m + 0.1 * g
    v = 0.95 * v + 0.05 * g * g
    step = m * lax.rsqrt(v + 1e-8) + 0.1 * w
    return (w - 0.02 * step).astype(jnp.bfloat16), m, v


def stack(weights, h):
    for number in range(weights["w_gate"].shape[0]):
        h = layer(h, {name: w[number] for name, w in weights.items()})
    return h


def solution(mesh):
    groups = mesh.shape["rep"]

    def step(x, dy, *arrays):
        weights, m, v = (arrays[i : i + 3] for i in (0, 3, 6))
        x, dy = (t.reshape(groups, -1, *t.shape[1:]) for t in (x, dy))

        def of_a_group(x, dy):
            _, back = jax.vjp(lambda w: stack(w, x), dict(zip(NAMES, weights, strict=True)))
            by_weights = back(dy)[0]
            gradients = [by_weights[name].astype(jnp.float32) for name in NAMES]
            new = [adamw(w.astype(jnp.float32), m, v, g) for w, m, v, g in zip(weights, m, v, gradients, strict=True)]
            return tuple(one[which] for which in range(3) for one in new)

        return tuple(t.reshape(-1, *t.shape[2:]) for t in jax.vmap(of_a_group)(x, dy))

    return step
```

profile of v0, /device:TPU:0, one launch (start us, length us, event | category | flops | bytes accessed | tf_op | source)
XLA Modules:
  0.0 1866.4 jit_solution(11774789733357502854)
XLA Ops:
  20.1 19.6 %fusion.173 = f32[2048,2816]{1,0:T(8,128)} fusion(bf16[2,1024,2816]{2,1,0:T(8,128)(2,1)} %param.12, bf16[1,2048,1024]{1,2,0:T(8,128)(2,1)S(1)} %fusion.157), kind=kOutput, calls=%fused_computation.224 | convolution fusion | flops 11811160064 | bytes 33030144 | tf_op jit(solution)/vmap(jvp())/dot_general | solution.py:20
  39.6 26.6 %fusion.150 = (bf16[1,2048,2816]{2,1,0:T(8,128)(2,1)}, f32[2048,2816]{1,0:T(8,128)}) fusion(f32[2048,2816]{1,0:T(8,128)} %fusion.173, bf16[2,1024,2816]{2,1,0:T(8,128)(2,1)} %param.17, bf16[1,2048,1024]{1,2,0:T(8,128)(2,1)S(1)} %fusion.157), kind=kOutput, calls=%fused_computation.189 | convolution fusion | flops 11845763072 | bytes 67633152 | tf_op jit(solution)/vmap(jvp())/dot_general | solution.py:21
  66.3 19.6 %fusion.160 = (f32[2048]{0:T(1024)S(1)}, bf16[1,2048,1024]{1,2,0:T(8,128)(2,1)}) fusion(bf16[1,2048,1024]{1,2,0:T(8,128)(2,1)} %copy.1, bf16[2,2816,1024]{2,1,0:T(8,128)(2,1)} %param.15, bf16[1,2048,2816]{2,1,0:T(8,128)(2,1)} %get-tuple-element.263), kind=kOutput, calls=%fused_computation.211 | convolution fusion | flops 11821643776 | bytes 25698304 | tf_op jit(solution)/vmap(jvp())/dot_general | solution.py:9
  89.8 19.6 %fusion.163 = f32[2048,2816]{1,0:T(8,128)} fusion(bf16[2,1024,2816]{2,1,0:T(8,128)(2,1)} %param.12, bf16[1,2048,1024]{1,2,0:T(8,128)(2,1)S(1)} %fusion.161), kind=kOutput, calls=%fused_computation.214 | convolution fusion | flops 11811160064 | bytes 33030144 | tf_op jit(solution)/vmap(jvp())/dot_general | solution.py:20
  109.4 27.1 %fusion.149 = (bf16[1,2048,2816]{2,1,0:T(8,128)(2,1)}, f32[2048,2816]{1,0:T(8,128)}) fusion(f32[2048,2816]{1,0:T(8,128)} %fusion.163, bf16[2,1024,2816]{2,1,0:T(8,128)(2,1)} %param.17, bf16[1,2048,1024]{1,2,0:T(8,128)(2,1)S(1)} %fusion.161), kind=kOutput, calls=%fused_computation.187 | convolution fusion | flops 11845763072 | bytes 67633152 | tf_op jit(solution)/vmap(jvp())/dot_general | solution.py:21
  136.5 15.3 copy.3
  151.8 231.3 %while.16 = (bf16[1,2048,2816]{1,2,0:T(8,128)(2,1)}, bf16[1,2048,1024]{2,1,0:T(8,128)(2,1)}, f32[88,1024]{1,0:T(8,128)S(1)}, f32[88,1024]{1,0:T(8,128)}, u32[]{:...) while((bf16[1,2048,2816]{1,2,0:T(8,128)(2,1)}, ...), condition=%wide.windowed_dot_general_cond_rs.4.clone, body=%wide.windowed_dot_general_body_rs.4.clone.sunk | while | flops 1479819264 | bytes 107348616 | solution.py:9
  389.8 15.2 copy.5
  405.1 33.6 %convert_multiply_fusion.2 = (bf16[1,2048,2816]{2,1,0:T(8,128)(2,1)}, bf16[1,2048,2816]{2,1,0:T(8,128)(2,1)}) fusion(f32[2048,2816]{1,0:T(8,128)} %fusion.163, f32[2048,2816]{1,0:T(8,128)} %get-tuple-element.270, bf16[2,2816,1024]{2,1,0:T(8,128)(2,1)} %param.15, bf16[1,2048,1024]{2,1,0:T(8,128)(2,1)} %get-tuple-element.744), kind=kOutput, calls=%fused_computation.170 | convolution fusion | flops 11903434752 | bytes 79167488 | tf_op jit(solution)/vmap(transpose(jvp()))/dot_general | solution.py:9
  438.7 18.1 fusion.142
  456.8 19.1 %fusion.162 = (f32[2048]{0:T(1024)S(1)}, bf16[2048,1024]{0,1:T(8,128)(2,1)}) fusion(bf16[1,2048,1024]{1,2,0:T(8,128)(2,1)S(1)} %copy-done.14, bf16[2048,1024]{0,1:T(8,128)(2,1)} %fusion.142, bf16[2,1024,2816]{2,1,0:T(8,128)(2,1)} %param.17, bf16[1,2048,2816]{2,1,0:T(8,128)(2,1)} %get-tuple-element.613), kind=kOutput, calls=%fused_computation.213 | convolution fusion | flops 11821643776 | bytes 29892608 | tf_op jit(solution)/vmap(transpose(jvp()))/dot_general | solution.py:21
  488.7 233.5 %while.17 = (bf16[1,2048,1024]{2,1,0:T(8,128)(2,1)}, bf16[1,2048,2816]{1,2,0:T(8,128)(2,1)}, f32[1024,88]{0,1:T(8,128)S(1)}, f32[1024,88]{0,1:T(8,128)}, u32[]{:...) while((bf16[1,2048,1024]{2,1,0:T(8,128)(2,1)}, ...), condition=%wide.windowed_dot_general_cond_rs.5.clone, body=%wide.windowed_dot_general_body_rs.5.clone.sunk | while | flops 1479819264 | bytes 107348616 | solution.py:9
  723.0 241.5 %while.14 = (bf16[1,2048,2816]{2,1,0:T(8,128)(2,1)}, bf16[1,2048,1024]{1,2,0:T(8,128)(2,1)}, f32[2816,32]{0,1:T(8,128)S(1)}, f32[2816,32]{0,1:T(8,128)}, u32[]{:...) while((bf16[1,2048,2816]{2,1,0:T(8,128)(2,1)}, ...), condition=%wide.windowed_dot_general_cond_rs.2.clone, body=%wide.windowed_dot_general_body_rs.2.clone.sunk | while | flops 1477984256 | bytes 107348616 | solution.py:21
  964.5 34.3 %convert_multiply_fusion = (bf16[1,2048,2816]{2,1,0:T(8,128)(2,1)}, bf16[1,2048,2816]{2,1,0:T(8,128)(2,1)}) fusion(f32[2048,2816]{1,0:T(8,128)} %fusion.173, f32[2048,2816]{1,0:T(8,128)} %get-tuple-element.264, bf16[2,2816,1024]{2,1,0:T(8,128)(2,1)} %param.15, bf16[1,2048,1024]{1,2,0:T(8,128)(2,1)} %fusion.185), kind=kOutput, calls=%fused_computation.168 | convolution fusion | flops 11903434752 | bytes 79167488 | tf_op jit(solution)/vmap(transpose(jvp()))/dot_general | solution.py:9
  998.8 220.8 %while.15 = (bf16[1,2048,2816]{2,1,0:T(8,128)(2,1)}, bf16[1,2048,1024]{1,2,0:T(8,128)(2,1)}, f32[2816,32]{0,1:T(8,128)S(1)}, f32[2816,32]{0,1:T(8,128)S(1)}, u32...) while((bf16[1,2048,2816]{2,1,0:T(8,128)(2,1)}, ...), condition=%wide.windowed_dot_general_cond_rs.3.clone, body=%wide.windowed_dot_general_body_rs.3.clone.sunk | while | flops 1477984256 | bytes 107348616 | solution.py:21
  1224.7 253.9 %while.12 = (bf16[1,2048,2816]{2,1,0:T(8,128)(2,1)}, bf16[1,2048,1024]{1,2,0:T(8,128)(2,1)}, f32[2816,32]{0,1:T(8,128)S(1)}, f32[2816,32]{0,1:T(8,128)S(1)}, u32...) while((bf16[1,2048,2816]{2,1,0:T(8,128)(2,1)}, ...), condition=%wide.windowed_dot_general_cond_rs.clone, body=%wide.windowed_dot_general_body_rs.clone.sunk | while | flops 1477984256 | bytes 107348616 | solution.py:20
  1246.5 12.2 collective-permute-done.2
  1309.0 9.7 collective-permute-done
  1326.4 13.7 collective-permute-done.2
  1483.7 251.9 %while.13 = (bf16[1,2048,2816]{2,1,0:T(8,128)(2,1)}, bf16[1,2048,1024]{1,2,0:T(8,128)(2,1)}, f32[2816,32]{0,1:T(8,128)S(1)}, f32[2816,32]{0,1:T(8,128)S(1)}, u32...) while((bf16[1,2048,2816]{2,1,0:T(8,128)(2,1)}, ...), condition=%wide.windowed_dot_general_cond_rs.1.clone, body=%wide.windowed_dot_general_body_rs.1.clone.sunk | while | flops 1477984256 | bytes 107348616 | solution.py:20
  1564.7 9.8 collective-permute-done.4
  1582.0 14.4 collective-permute-done.6
  1749.0 86.7 %all-gather.10.cloned.1.call-done = bf16[1,2,1024,2816]{3,2,1,0:T(8,128)(2,1)} async-done(((bf16[1,2,32,2816]{3,2,1,0:T(8,128)(2,1)}), bf16[1,2,1024,2816]{3,2,1,0:T(8,128)(2,1)}) %all-gather.10.cloned.1.call-update) | async-done | bytes 11534352 | tf_op jit(solution)/reshape | solution.py:52
  1835.7 11.7 copy.63
  (958 shorter events, 1443.0 us)
Async XLA Ops:
  7.2 1741.8 %all-gather.14.cloned.1.call-start = ((), (), s32[]{:S(2)}) async-start(), calls=%async_computation.2 | async-start | bytes 11894784 | tf_op jit(solution)/reshape | solution.py:52
  383.1 836.5 %collective-permute-start.28 = (f32[88,1024]{1,0:T(8,128)}, f32[88,1024]{1,0:T(8,128)}, u32[]{:S(2)}, u32[]{:S(2)}) collective-permute-start(f32[88,1024]{1,0:T(8,128)} %get-tuple-element.45), channel_id=32, source_target_pairs={{0,1},{1,2},{2,3},{3,4},{4,5},{5,6},{6,7},{7,8},{8,9},{9,10},{10,1... | collective-permute-start | bytes 1081352 | tf_op jit(solution)/vmap(transpose(jvp()))/dot_general | solution.py:9
  722.2 498.5 %collective-permute-start.29 = (f32[1024,88]{0,1:T(8,128)}, f32[1024,88]{0,1:T(8,128)}, u32[]{:S(2)}, u32[]{:S(2)}) collective-permute-start(f32[1024,88]{0,1:T(8,128)} %get-tuple-element.47), channel_id=38, source_target_pairs={{0,1},{1,2},{2,3},{3,4},{4,5},{5,6},{6,7},{7,8},{8,9},{9,10},{10,1... | collective-permute-start | bytes 1081352 | tf_op jit(solution)/vmap(transpose(jvp()))/dot_general | solution.py:9
  723.0 17.5 collective-permute-start.8
  723.1 17.4 collective-permute-start.9
  964.5 514.2 %collective-permute-start.26 = (f32[2816,32]{0,1:T(8,128)}, f32[2816,32]{0,1:T(8,128)}, u32[]{:S(2)}, u32[]{:S(2)}) collective-permute-start(f32[2816,32]{0,1:T(8,128)} %get-tuple-element.41), channel_id=19, source_target_pairs={{0,1},{1,2},{2,3},{3,4},{4,5},{5,6},{6,7},{7,8},{8,9},{9,10},{10,1... | collective-permute-start | bytes 1081352 | tf_op jit(solution)/vmap(transpose(jvp()))/dot_general | solution.py:21
  1219.6 260.1 %collective-permute-start.27 = (f32[2816,32]{0,1:T(8,128)S(1)}, f32[2816,32]{0,1:T(8,128)}, u32[]{:S(2)}, u32[]{:S(2)}) collective-permute-start(f32[2816,32]{0,1:T(8,128)S(1)} %get-tuple-element.43), channel_id=25, source_target_pairs={{0,1},{1,2},{2,3},{3,4},{4,5},{5,6},{6,7},{7,8},{8,9},{9,10},{10,1... | collective-permute-start | bytes 1081352 | tf_op jit(solution)/vmap(transpose(jvp()))/dot_general | solution.py:21
  1224.6 524.4 %all-gather.12.cloned.1.call-start = ((), (), s32[]{:S(2)}) async-start(), calls=%async_computation.1 | async-start | bytes 11894784 | tf_op jit(solution)/reshape | solution.py:52
  1238.7 20.0 %collective-permute-start.2 = (f32[2816,32]{0,1:T(8,128)S(1)}, f32[2816,32]{0,1:T(8,128)S(1)}, u32[]{:S(2)}, u32[]{:S(2)}) collective-permute-start(f32[2816,32]{0,1:T(8,128)S(1)} %get-tuple-element.456), channel_id=5, source_target_pairs={{0,1},{1,2},{2,3},{3,4},{4,5},{5,6},{6,7},{7,8},{8,9},{9,10},{10,1... | collective-permute-start | bytes 1081352 | tf_op jit(solution)/vmap(transpose(jvp()))/dot_general | solution.py:20
  1238.8 19.9 %collective-permute-start.3 = (f32[2816,32]{0,1:T(8,128)S(1)}, f32[2816,32]{0,1:T(8,128)S(1)}, u32[]{:S(2)}, u32[]{:S(2)}) collective-permute-start(f32[2816,32]{0,1:T(8,128)S(1)} %get-tuple-element.457), channel_id=4, source_target_pairs={{0,31},{1,0},{2,1},{3,2},{4,3},{5,4},{6,5},{7,6},{8,7},{9,8},{10,9... | collective-permute-start | bytes 1081352 | tf_op jit(solution)/vmap(transpose(jvp()))/dot_general | solution.py:20
  1258.8 20.1 %collective-permute-start = (f32[2816,32]{0,1:T(8,128)S(1)}, f32[2816,32]{0,1:T(8,128)S(1)}, u32[]{:S(2)}, u32[]{:S(2)}) collective-permute-start(f32[2816,32]{0,1:T(8,128)S(1)} %broadcast_select_fusion.24), channel_id=3, source_target_pairs={{0,1},{1,2},{2,3},{3,4},{4,5},{5,6},{6,7},{7,8},{8,9},{9,10},{10,1... | collective-permute-start | bytes 1081352 | tf_op jit(solution)/vmap(transpose(jvp()))/dot_general | solution.py:20
  1258.9 21.1 %collective-permute-start.1 = (f32[2816,32]{0,1:T(8,128)S(1)}, f32[2816,32]{0,1:T(8,128)S(1)}, u32[]{:S(2)}, u32[]{:S(2)}) collective-permute-start(f32[2816,32]{0,1:T(8,128)S(1)} %broadcast_select_fusion.25), channel_id=2, source_target_pairs={{0,31},{1,0},{2,1},{3,2},{4,3},{5,4},{6,5},{7,6},{8,7},{9,8},{10,9... | collective-permute-start | bytes 1081352 | tf_op jit(solution)/vmap(transpose(jvp()))/dot_general | solution.py:20
  1296.7 22.0 %collective-permute-start = (f32[2816,32]{0,1:T(8,128)S(1)}, f32[2816,32]{0,1:T(8,128)S(1)}, u32[]{:S(2)}, u32[]{:S(2)}) collective-permute-start(f32[2816,32]{0,1:T(8,128)S(1)} %broadcast_select_fusion.24), channel_id=3, source_target_pairs={{0,1},{1,2},{2,3},{3,4},{4,5},{5,6},{6,7},{7,8},{8,9},{9,10},{10,1... | collective-permute-start | bytes 1081352 | tf_op jit(solution)/vmap(transpose(jvp()))/dot_general | solution.py:20
  1296.8 21.9 %collective-permute-start.1 = (f32[2816,32]{0,1:T(8,128)S(1)}, f32[2816,32]{0,1:T(8,128)S(1)}, u32[]{:S(2)}, u32[]{:S(2)}) collective-permute-start(f32[2816,32]{0,1:T(8,128)S(1)} %broadcast_select_fusion.25), channel_id=2, source_target_pairs={{0,31},{1,0},{2,1},{3,2},{4,3},{5,4},{6,5},{7,6},{8,7},{9,8},{10,9... | collective-permute-start | bytes 1081352 | tf_op jit(solution)/vmap(transpose(jvp()))/dot_general | solution.py:20
  1318.8 21.2 %collective-permute-start.2 = (f32[2816,32]{0,1:T(8,128)S(1)}, f32[2816,32]{0,1:T(8,128)S(1)}, u32[]{:S(2)}, u32[]{:S(2)}) collective-permute-start(f32[2816,32]{0,1:T(8,128)S(1)} %get-tuple-element.456), channel_id=5, source_target_pairs={{0,1},{1,2},{2,3},{3,4},{4,5},{5,6},{6,7},{7,8},{8,9},{9,10},{10,1... | collective-permute-start | bytes 1081352 | tf_op jit(solution)/vmap(transpose(jvp()))/dot_general | solution.py:20
  1318.9 21.1 %collective-permute-start.3 = (f32[2816,32]{0,1:T(8,128)S(1)}, f32[2816,32]{0,1:T(8,128)S(1)}, u32[]{:S(2)}, u32[]{:S(2)}) collective-permute-start(f32[2816,32]{0,1:T(8,128)S(1)} %get-tuple-element.457), channel_id=4, source_target_pairs={{0,31},{1,0},{2,1},{3,2},{4,3},{5,4},{6,5},{7,6},{8,7},{9,8},{10,9... | collective-permute-start | bytes 1081352 | tf_op jit(solution)/vmap(transpose(jvp()))/dot_general | solution.py:20
  1478.6 257.0 %collective-permute-start.24 = (f32[2816,32]{0,1:T(8,128)S(1)}, f32[2816,32]{0,1:T(8,128)}, u32[]{:S(2)}, u32[]{:S(2)}) collective-permute-start(f32[2816,32]{0,1:T(8,128)S(1)} %get-tuple-element.37), channel_id=6, source_target_pairs={{0,1},{1,2},{2,3},{3,4},{4,5},{5,6},{6,7},{7,8},{8,9},{9,10},{10,1... | collective-permute-start | bytes 1081352 | tf_op jit(solution)/vmap(transpose(jvp()))/dot_general | solution.py:20
  1483.6 352.1 %all-gather.10.cloned.1.call-start = ((), (), s32[]{:S(2)}) async-start(), calls=%async_computation | async-start | bytes 11894784 | tf_op jit(solution)/reshape | solution.py:52
  1516.5 21.3 %collective-permute-start.4 = (f32[2816,32]{0,1:T(8,128)S(1)}, f32[2816,32]{0,1:T(8,128)S(1)}, u32[]{:S(2)}, u32[]{:S(2)}) collective-permute-start(f32[2816,32]{0,1:T(8,128)S(1)} %broadcast_select_fusion.26), channel_id=9, source_target_pairs={{0,1},{1,2},{2,3},{3,4},{4,5},{5,6},{6,7},{7,8},{8,9},{9,10},{10,1... | collective-permute-start | bytes 1081352 | tf_op jit(solution)/vmap(transpose(jvp()))/dot_general | solution.py:20
  1516.6 21.4 %collective-permute-start.5 = (f32[2816,32]{0,1:T(8,128)S(1)}, f32[2816,32]{0,1:T(8,128)S(1)}, u32[]{:S(2)}, u32[]{:S(2)}) collective-permute-start(f32[2816,32]{0,1:T(8,128)S(1)} %broadcast_select_fusion.27), channel_id=8, source_target_pairs={{0,31},{1,0},{2,1},{3,2},{4,3},{5,4},{6,5},{7,6},{8,7},{9,8},{10,9... | collective-permute-start | bytes 1081352 | tf_op jit(solution)/vmap(transpose(jvp()))/dot_general | solution.py:20
  1552.5 21.9 %collective-permute-start.4 = (f32[2816,32]{0,1:T(8,128)S(1)}, f32[2816,32]{0,1:T(8,128)S(1)}, u32[]{:S(2)}, u32[]{:S(2)}) collective-permute-start(f32[2816,32]{0,1:T(8,128)S(1)} %broadcast_select_fusion.26), channel_id=9, source_target_pairs={{0,1},{1,2},{2,3},{3,4},{4,5},{5,6},{6,7},{7,8},{8,9},{9,10},{10,1... | collective-permute-start | bytes 1081352 | tf_op jit(solution)/vmap(transpose(jvp()))/dot_general | solution.py:20
  1552.6 21.8 %collective-permute-start.5 = (f32[2816,32]{0,1:T(8,128)S(1)}, f32[2816,32]{0,1:T(8,128)S(1)}, u32[]{:S(2)}, u32[]{:S(2)}) collective-permute-start(f32[2816,32]{0,1:T(8,128)S(1)} %broadcast_select_fusion.27), channel_id=8, source_target_pairs={{0,31},{1,0},{2,1},{3,2},{4,3},{5,4},{6,5},{7,6},{8,7},{9,8},{10,9... | collective-permute-start | bytes 1081352 | tf_op jit(solution)/vmap(transpose(jvp()))/dot_general | solution.py:20
  1574.5 21.9 %collective-permute-start.6 = (f32[2816,32]{0,1:T(8,128)S(1)}, f32[2816,32]{0,1:T(8,128)S(1)}, u32[]{:S(2)}, u32[]{:S(2)}) collective-permute-start(f32[2816,32]{0,1:T(8,128)S(1)} %get-tuple-element.465), channel_id=11, source_target_pairs={{0,1},{1,2},{2,3},{3,4},{4,5},{5,6},{6,7},{7,8},{8,9},{9,10},{10,1... | collective-permute-start | bytes 1081352 | tf_op jit(solution)/vmap(transpose(jvp()))/dot_general | solution.py:20
  1574.6 21.8 %collective-permute-start.7 = (f32[2816,32]{0,1:T(8,128)S(1)}, f32[2816,32]{0,1:T(8,128)S(1)}, u32[]{:S(2)}, u32[]{:S(2)}) collective-permute-start(f32[2816,32]{0,1:T(8,128)S(1)} %get-tuple-element.466), channel_id=10, source_target_pairs={{0,31},{1,0},{2,1},{3,2},{4,3},{5,4},{6,5},{7,6},{8,7},{9,8},{10,9... | collective-permute-start | bytes 1081352 | tf_op jit(solution)/vmap(transpose(jvp()))/dot_general | solution.py:20
  (295 other events, 5472.3 us)
Sparse Core Ops, SparseCore 0:
  1224.7 113.0 all-gather.13
  1483.7 115.4 all-gather.11
  1749.1 86.5 all-gather.9
where the time goes:
time: 1880 us; the launch traced here: 1870 us
  waiting for transfers between devices  602 us (32%)
  matrix products  567 us (30%)
  starting transfers between devices  525 us (28%)
  other arithmetic  79.8 us (4%)
  local copies, waits for them, and re-layouts  75.8 us (4%)
    dot_general x35, matrix products, layer(): up = jnp.dot(a, w['w_up'], preferred_element_type=jnp.float32)  212 us
    dot_general x35, matrix products, layer(): gate = jnp.dot(a, w['w_gate'], preferred_element_type=jnp.float32)  197 us
    dot_general x66, waiting for transfers between devices, layer(): gate = jnp.dot(a, w['w_gate'], preferred_element_type=jnp.float32)  195 us
    dot_general x66, waiting for transfers between devices, matmul(): jnp.dot(a, w, preferred_element_type=jnp.float32).astype(jnp.bfloat16)  189 us
    dot_general x66, starting transfers between devices, layer(): gate = jnp.dot(a, w['w_gate'], preferred_element_type=jnp.float32)  176 us
    dot_general x66, starting transfers between devices, layer(): up = jnp.dot(a, w['w_up'], preferred_element_type=jnp.float32)  174 us
    dot_general x66, starting transfers between devices, matmul(): jnp.dot(a, w, preferred_element_type=jnp.float32).astype(jnp.bfloat16)  174 us
    dot_general x35, matrix products, matmul(): jnp.dot(a, w, preferred_element_type=jnp.float32).astype(jnp.bfloat16)  158 us
  transfers between devices with their start and end apart: 201, of which 111 were waited for; matrix products, arithmetic and copies ran while one was open for 29% of the time, Pallas kernels for 0%

commit v1 on v0

v1 whole, which is shorter than its diff:
```python
import jax
import jax.numpy as jnp
from jax import lax
from jax.experimental import pallas as pl
from jax.experimental.pallas import tpu as pltpu
from jax.sharding import PartitionSpec as P

F32, BF16 = jnp.float32, jnp.bfloat16
AXES = "dp"


DIMS = {"x": 16, "y": 8, "b": 4, "a": 2, "c": 1}
LEAD = "xyba"
PARTS = {
    2816: ((0, 1152, "xyab"), (1152, 2304, "yxab"), (2304, 2816, "abxy")),
    1024: ((0, 384, "xyab"), (384, 768, "yxab"), (768, 1024, "abyx")),
}
STEP = {32: 384, 88: 128}


def place():
    me = lax.axis_index(AXES)
    own = {d: (me // s) % 2 for d, s in DIMS.items()}
    peer = {d: me + (1 - 2 * own[d]) * s for d, s in DIMS.items()}
    return own, peer


def greet(peer):
    barrier = pltpu.get_barrier_semaphore()
    for d in DIMS:
        pl.semaphore_signal(barrier, inc=1, device_id={AXES: peer[d]}, device_id_type=pl.DeviceIdType.MESH)
    pl.semaphore_wait(barrier, len(DIMS))


def remote(src, dst, sems, n, target):
    return pltpu.make_async_remote_copy(
        src_ref=src, dst_ref=dst, send_sem=sems[0].at[n], recv_sem=sems[1].at[n], device_id={AXES: target}, device_id_type=pl.DeviceIdType.MESH
    )


def steps_of(lo, hi, rows):
    step = STEP[rows]
    return [(at, min(step, hi - at)) for at in range(lo, hi, step)]


def in_turn(steps, count):
    return sorted(((k, i) for k in range(steps) for i in range(count)), key=lambda at: 1.5 * at[0] + at[1])


class Scatter:
    def __init__(self, grad, held, came, later, out, sems, local, first, own, peer):
        self.grad, self.held, self.came, self.later, self.out = grad, held, came, later, out
        self.own, self.peer = own, peer
        self.rows, self.cols = grad.shape[-2:]
        self.parts = PARTS[self.cols]
        self.copies, n = {}, first
        for p, (lo, hi, order) in enumerate(self.parts):
            for half in range(2):
                at = tuple((1 - own[d] if half == 0 else own[d]) if d == order[0] else slice(None) for d in LEAD)
                here = at + (slice(None), pl.ds(lo, hi - lo))
                mine, theirs = at + (own["c"], slice(None), pl.ds(lo, hi - lo)), at + (1 - own["c"], slice(None), pl.ds(lo, hi - lo))
                self.copies["c", p, half] = remote(grad.at[theirs], came.at[here], sems, n, peer["c"])
                self.copies["own", p, half] = pltpu.make_async_copy(grad.at[mine], held.at[here], local.at[n])
                n += 1
            for k, d in enumerate(order):
                at = tuple(own[e] if e in order[:k] else 1 - own[e] if e == d else slice(None) for e in LEAD)
                self.copies[k, p] = remote(held.at[at + (slice(None), pl.ds(lo, hi - lo))], later[p][k], sems, n, peer[d])
                n += 1
        self.used = n - first

    def begin(self, half):
        for p in range(len(self.parts)):
            self.copies["c", p, half].start()
            self.copies["own", p, half].start()

    def add(self, p, k):
        lo, hi, order = self.parts[p]
        free = order[k + 1 :]

        def block(i, _):
            at = {}
            for n, e in enumerate(order):
                at[e] = self.own[e] if n < k else 1 - self.own[e] if n == k else (i // 2 ** (len(order) - 1 - n)) % 2
            lead = tuple(at[e] for e in LEAD)
            for c, size in steps_of(lo, hi, self.rows):
                here = lead + (slice(None), pl.ds(c, size))
                total = self.held[here].astype(F32) + self.came[here].astype(F32)
                for j in range(min(k, len(order))):
                    inner = tuple(at[e] for e in LEAD if e in order[j + 1 :])
                    total = total + self.later[p][j][inner + (slice(None), pl.ds(c - lo, size))].astype(F32)
                if k < len(order):
                    self.held[here] = total.astype(BF16)
                else:
                    self.out[:, pl.ds(c, size)] = total.astype(BF16)
            return 0

        if len(free) == 0:
            block(0, 0)
        else:
            lax.fori_loop(0, 2 ** len(free), block, 0)

    def send(self, p, k):
        if k == 0:
            self.copies["c", p, 0].wait_recv()
            self.copies["own", p, 0].wait()
        else:
            if k == 1:
                self.copies["c", p, 1].wait_recv()
                self.copies["own", p, 1].wait()
            self.copies[k - 1, p].wait_recv()
        self.add(p, k)
        if k < 4:
            self.copies[k, p].start()

    def finish(self):
        for name, copy in self.copies.items():
            if name[0] != "own":
                copy.wait_send()


def copies_of(cols):
    return len(PARTS[cols]) * 6


def later_shapes(rows, cols):
    return [[pltpu.VMEM((2,) * (3 - k) + (rows, hi - lo), BF16) for k in range(4)] for lo, hi, _ in PARTS[cols]]


def scatter(grads, collective_id):
    shapes = [g.shape for g in grads]
    shapes = [(s[0] // 32, s[1]) for s in shapes]
    count = len(shapes)

    def kernel(*refs):
        refs = list(refs)
        ins, outs = refs[:count], refs[count : 2 * count]
        held, came, later, sems, local = refs[2 * count :]
        own, peer = place()
        greet(peer)
        work, n = [], 0
        for i in range(count):
            work.append(Scatter(ins[i], held[i], came[i], later[i], outs[i], sems, local, n, own, peer))
            n += work[-1].used
        for half in range(2):
            for w in work:
                w.begin(half)
        for k, i in in_turn(5, count):
            for p in range(len(work[i].parts)):
                work[i].send(p, k)
        for w in work:
            w.finish()

    total = sum(copies_of(c) for _, c in shapes)
    return pl.pallas_call(
        kernel,
        name="scatter",
        out_shape=[jax.ShapeDtypeStruct(s, BF16) for s in shapes],
        in_specs=[pl.BlockSpec(memory_space=pl.ANY)] * count,
        out_specs=[pl.BlockSpec(memory_space=pltpu.VMEM)] * count,
        scratch_shapes=[
            [pltpu.VMEM((2, 2, 2, 2) + s, BF16) for s in shapes],
            [pltpu.VMEM((2, 2, 2, 2) + s, BF16) for s in shapes],
            [later_shapes(*s) for s in shapes],
            [pltpu.SemaphoreType.DMA((total,)), pltpu.SemaphoreType.DMA((total,))],
            pltpu.SemaphoreType.DMA((total,)),
        ],
        compiler_params=pltpu.CompilerParams(collective_id=collective_id, has_side_effects=True, vmem_limit_bytes=60 * 2**20),
    )(*(g.reshape((2,) * 5 + s) for g, s in zip(grads, shapes)))


def gather(blocks, collective_id):
    count = len(blocks)
    layers = blocks[0].shape[0]
    total = layers * sum(len(PARTS[b.shape[2]]) * 5 for b in blocks)

    def kernel(*refs):
        ins, outs = refs[:count], refs[count : 2 * count]
        send, recv, local = refs[2 * count :]
        own, peer = place()
        mine = tuple(own[e] for e in LEAD)
        every = slice(None)
        keep = [pltpu.make_async_copy(ins[i], outs[i].at[(every,) + mine + (own["c"],)], local.at[i]) for i in range(count)]
        for copy in keep:
            copy.start()
        greet(peer)
        copies, n = {}, 0
        units = [(layer, i) for layer in reversed(range(layers)) for i in range(count)]
        for u, (layer, i) in enumerate(units):
            for p, (lo, hi, order) in enumerate(PARTS[outs[i].shape[-1]]):
                cols = (every, pl.ds(lo, hi - lo))
                for k, d in enumerate(order[::-1] + "c"):
                    got = order[::-1][:k]
                    at = (layer,) + tuple(every if e in got else own[e] for e in LEAD) + (own["c"],) + cols
                    src = ins[i].at[(layer,) + cols] if k == 0 else outs[i].at[at]
                    copies[u, p, k] = remote(src, outs[i].at[at], (send, recv), n, peer[d])
                    n += 1
        kept = set()
        for k, u in in_turn(5, len(units)):
            i = units[u][1]
            if k == 1 and i not in kept:
                kept.add(i)
                keep[i].wait()
            for p in range(len(PARTS[outs[i].shape[-1]])):
                if k:
                    copies[u, p, k - 1].wait_recv()
                copies[u, p, k].start()
        for (u, p, k), copy in copies.items():
            if k == 4:
                copy.wait_recv()
            copy.wait_send()

    outs = pl.pallas_call(
        kernel,
        name="gather",
        out_shape=[jax.ShapeDtypeStruct((layers,) + (2,) * 5 + b.shape[1:], BF16) for b in blocks],
        in_specs=[pl.BlockSpec(memory_space=pl.ANY)] * count,
        out_specs=[pl.BlockSpec(memory_space=pl.ANY)] * count,
        scratch_shapes=[pltpu.SemaphoreType.DMA((total,)), pltpu.SemaphoreType.DMA((total,)), pltpu.SemaphoreType.DMA((count,))],
        compiler_params=pltpu.CompilerParams(collective_id=collective_id, has_side_effects=True),
    )(*blocks)
    return [o.reshape(layers, -1, o.shape[-1]) for o in outs]


def dot(a, b, contract):
    return lax.dot_general(a, b, ((contract[:1], contract[1:]), ((), ())), preferred_element_type=F32)


def norm_scale(h):
    wide = h.astype(F32)
    return lax.rsqrt(jnp.mean(wide**2, -1, keepdims=True) + 1e-6)


def adamw(w, m, v, g):
    m = 0.9 * m + 0.1 * g
    v = 0.95 * v + 0.05 * g * g
    step = m * lax.rsqrt(v + 1e-8) + 0.1 * w
    return (w - 0.02 * step).astype(BF16), m, v


def silu_parts(gate):
    s = jax.nn.sigmoid(gate)
    return gate * s, s * (1 + gate * (1 - s))


def body(x, dy, wg, wu, wd, mg, mu, md, vg, vu, vd):
    x, dy = x[0], dy[0]
    a0 = (x.astype(F32) * norm_scale(x)).astype(BF16)
    g0 = dot(a0, wg[0], (1, 0))
    u0 = dot(a0, wu[0], (1, 0))
    p0 = (jax.nn.silu(g0) * u0).astype(BF16)
    h1 = x + dot(p0, wd[0], (1, 0)).astype(BF16)
    r1 = norm_scale(h1)
    a1 = (h1.astype(F32) * r1).astype(BF16)
    g1 = dot(a1, wg[1], (1, 0))
    u1 = dot(a1, wu[1], (1, 0))

    def back(a, p, g, u, d, wdl):
        dp = dot(d, wdl, (1, 1)).astype(BF16).astype(F32)
        s, ds = silu_parts(g)
        dwd = dot(p, d, (0, 0)).astype(BF16)
        dg = (dp * u * ds).astype(BF16)
        du = (dp * s).astype(BF16)
        return dg, du, dot(a, dg, (0, 0)).astype(BF16), dot(a, du, (0, 0)).astype(BF16), dwd

    p1 = (jax.nn.silu(g1) * u1).astype(BF16)
    dg1, du1, dwg1, dwu1, dwd1 = back(a1, p1, g1, u1, dy, wd[1])
    da1 = (dot(dg1, wg[1], (1, 1)).astype(BF16) + dot(du1, wu[1], (1, 1)).astype(BF16)).astype(F32)
    wide = h1.astype(F32)
    inner = jnp.sum(da1 * wide, -1, keepdims=True) / wide.shape[-1]
    dnorm = (da1 * r1 - wide * (r1 * r1 * r1) * inner).astype(BF16)
    dh1 = dy + dnorm
    dg0, du0, dwg0, dwu0, dwd0 = back(a0, p0, g0, u0, dh1, wd[0])
    i = lax.axis_index(AXES)
    sums1 = scatter([dwd1, dwg1, dwu1], 0)
    sums0 = scatter([dwd0, dwg0, dwu0], 1)
    new = []
    for w, m, v, one, two in ((wd, md, vd, sums0[0], sums1[0]), (wg, mg, vg, sums0[1], sums1[1]), (wu, mu, vu, sums0[2], sums1[2])):
        n = m.shape[1]
        g = jnp.stack([one, two]).astype(F32)
        mine = lax.dynamic_slice_in_dim(w, i * n, n, 1).astype(F32)
        new.append(adamw(mine, m, v, g))
    nd, ng, nu = gather([n[0] for n in new], 2)
    down, gate, up = new
    return ng, nu, nd, gate[1], up[1], down[1], gate[2], up[2], down[2]


def solution(mesh):
    whole, seq, part = P(None, None, None), P(("rep", "dp"), None, None), P(None, "dp", None)
    outw, outm = P("rep", None, None), P("rep", "dp", None)
    return jax.shard_map(body, mesh=mesh, in_specs=(seq, seq) + (whole,) * 3 + (part,) * 6, out_specs=(outw,) * 3 + (outm,) * 6, check_vma=False)
```

time: 1880 us -> 704 us (0.37)
  waiting for transfers between devices: 602 us -> 0 us
  starting transfers between devices: 525 us -> 0 us
  Pallas kernels: 0 us -> 327 us
  matrix products: 567 us -> 316 us
  other arithmetic: 79.8 us -> 16.1 us
  local copies, waits for them, and re-layouts: 75.8 us -> 37 us
    dot_general x198 -> x0, starting transfers between devices: 525 us -> none  [the longest x66 176 us: layer(): gate = jnp.dot(a, w['w_gate'], preferred_element_type=jnp.float32)]
    dot_general x198 -> x0, waiting for transfers between devices: 515 us -> none  [the longest x66 195 us: layer(): gate = jnp.dot(a, w['w_gate'], preferred_element_type=jnp.float32)]
    pallas_call x0 -> x3, Pallas kernels: none -> 327 us  [the longest x2 173 us: scatter(): pl.pallas_call(kernel, name='scatter', out_shape=[jax.ShapeDtypeStruct(s,...]
    dot_general x105 -> x15, matrix products: 567 us -> 316 us  [dot(): lax.dot_general(a, b, ((contract[:1], contract[1:]), ((), ())), preferred...]
    reshape x3 -> x0, waiting for transfers between devices: 86.8 us -> none  [step(): t.reshape(-1, *t.shape[2:])]
    dot_general x192 -> x0, other arithmetic: 50.2 us -> none
    unnamed x52 -> x45, local copies, waits for them, and re-layouts: 75.4 us -> 37 us
  transfers between devices with their start and end apart: 201 -> 0, of which waited for: 111 -> 0; matrix products, arithmetic and copies ran while one was open for 29% -> 0% of each run, Pallas kernels for 0% -> 0%
where the time goes in v1:
time: 704 us; the launch traced here: 698 us
  Pallas kernels  327 us (46%)
  matrix products  316 us (45%)
  local copies, waits for them, and re-layouts  37 us (5%)
  other arithmetic  16.1 us (2%)
    dot_general x15, matrix products, dot(): lax.dot_general(a, b, ((contract[:1], contract[1:]), ((), ())), preferred...  316 us
    pallas_call x2, Pallas kernels, scatter(): pl.pallas_call(kernel, name='scatter', out_shape=[jax.ShapeDtypeStruct(s,...  173 us
    pallas_call x1, Pallas kernels, gather(): pl.pallas_call(kernel, name='gather', out_shape=[jax.ShapeDtypeStruct((la...  154 us
    unnamed x45, local copies, waits for them, and re-layouts  37 us

profile of v1, /device:TPU:0, one launch (start us, length us, event | category | flops | bytes accessed | tf_op | source)
XLA Modules:
  0.0 697.7 jit_solution(5630630368382408765)
XLA Ops:
  0.6 6.5 copy.20
  10.2 19.9 %fusion.35 = f32[2048,2816]{1,0:T(8,128)} fusion(bf16[2,1024,2816]{2,1,0:T(8,128)(2,1)} %param.13, bf16[1,2048,1024]{2,1,0:T(8,128)(2,1)} %param.11, f32[2048]{0:T(1024)S(1)} %add_rsqrt_fusion.1), kind=kOutput, calls=%fused_computation.51 | convolution fusion | flops 11817451520 | bytes 33038336 | tf_op jit(solution)/shard_map/dot_general | solution.py:225
  30.1 28.7 %multiply_convert_fusion.1 = (bf16[2048,2816]{1,0:T(8,128)(2,1)}, f32[2048,2816]{1,0:T(8,128)}) fusion(f32[2048,2816]{1,0:T(8,128)} %fusion.35, bf16[2,1024,2816]{2,1,0:T(8,128)(2,1)} %param.14, bf16[1,2048,1024]{2,1,0:T(8,128)(2,1)} %param.11, f32[2048]{0:T(1024)S(1)} %add_rsqrt_fusion.1), kind=kOutput, calls=%fused_computation.13 | convolution fusion | flops 11852054528 | bytes 67641344 | tf_op jit(solution)/shard_map/dot_general | solution.py:225
  58.8 19.9 %fusion.17 = (f32[2048]{0:T(1024)S(1)}, bf16[2048,1024]{0,1:T(8,128)(2,1)}) fusion(bf16[2048,2816]{1,0:T(8,128)(2,1)} %get-tuple-element.40, bf16[2,2816,1024]{2,1,0:T(8,128)(2,1)} %param.15, bf16[1,2048,1024]{1,2,0:T(8,128)(2,1)} %copy.20), kind=kOutput, calls=%fused_computation.32 | convolution fusion | flops 11821643776 | bytes 25698304 | tf_op jit(solution)/shard_map/dot_general | solution.py:225
  79.3 20.2 %fusion.27 = f32[2048,2816]{1,0:T(8,128)} fusion(bf16[2,1024,2816]{2,1,0:T(8,128)(2,1)} %param.14, bf16[2048,1024]{0,1:T(8,128)(2,1)} %get-tuple-element.43, f32[2048]{0:T(1024)S(1)} %get-tuple-element.39), kind=kOutput, calls=%fused_computation.43 | convolution fusion | flops 11817451520 | bytes 33038336 | tf_op jit(solution)/shard_map/dot_general | solution.py:225
  99.5 18.3 %fusion.23 = f32[2048,2816]{1,0:T(8,128)} fusion(bf16[2,1024,2816]{2,1,0:T(8,128)(2,1)} %param.13, bf16[2048,1024]{0,1:T(8,128)(2,1)S(1)} %copy-done.2, f32[2048]{0:T(1024)S(1)} %get-tuple-element.39), kind=kOutput, calls=%fused_computation.39 | convolution fusion | flops 11817451520 | bytes 33038336 | tf_op jit(solution)/shard_map/dot_general | solution.py:225
  117.8 23.6 %fusion.40 = bf16[2816,1024]{1,0:T(8,128)(2,1)} fusion(f32[2048,2816]{1,0:T(8,128)} %fusion.27, bf16[1,2048,1024]{2,1,0:T(8,128)(2,1)S(1)} %copy-done.5, f32[2048,2816]{1,0:T(8,128)} %fusion.23), kind=kOutput, calls=%fused_computation.56 | convolution fusion | flops 11848646656 | bytes 56098816 | tf_op jit(solution)/shard_map/dot_general | solution.py:225
  141.3 33.6 %fusion.2 = (bf16[2048,2816]{1,0:T(8,128)(2,1)}, bf16[2048,2816]{1,0:T(8,128)(2,1)}) fusion(f32[2048,2816]{1,0:T(8,128)} %fusion.23, f32[2048,2816]{1,0:T(8,128)} %fusion.27, bf16[2,2816,1024]{2,1,0:T(8,128)(2,1)} %param.15, bf16[1,2048,1024]{2,1,0:T(8,128)(2,1)} %param.12), kind=kOutput, calls=%fused_computation.6 | convolution fusion | flops 11897667584 | bytes 79167488 | tf_op jit(solution)/shard_map/dot_general | solution.py:225
  175.0 18.7 %convolution_convert_fusion.3 = bf16[1024,2816]{1,0:T(8,128)(2,1)} fusion(bf16[2048,2816]{1,0:T(8,128)(2,1)} %get-tuple-element.37, bf16[2048,1024]{0,1:T(8,128)(2,1)} %get-tuple-element.43, f32[2048]{0:T(1024)S(1)} %get-tuple-element.39), kind=kOutput, calls=%fused_computation.60 | convolution fusion | flops 11820335104 | bytes 21504000 | tf_op jit(solution)/shard_map/dot_general | solution.py:225
  193.7 14.4 %convolution_convert_fusion.2 = bf16[1024,2816]{1,0:T(8,128)(2,1)} fusion(bf16[2048,2816]{1,0:T(8,128)(2,1)S(1)} %copy-done.16, bf16[2048,1024]{0,1:T(8,128)(2,1)S(1)} %copy-done.3, f32[2048]{0:T(1024)S(1)} %get-tuple-element.39), kind=kOutput, calls=%fused_computation.59 | convolution fusion | flops 11820335104 | bytes 21504000 | tf_op jit(solution)/shard_map/dot_general | solution.py:225
  208.1 86.7 %scatter.3 = (bf16[88,1024]{1,0:T(8,128)(2,1)}, bf16[32,2816]{1,0:T(8,128)(2,1)}, bf16[32,2816]{1,0:T(8,128)(2,1)}) custom-call(bf16[2,2,2,2,2,88,1024]{6,5,4,3,2,1,0:T(8,128)(2,1)} %bitcast.87, bf16[2,2,2,2,2,32,2816]{6,5,4,3,2,1,0:T(8,128)(2,1)} %bitcast.90, bf16[2,2,2,2,2,32,2816]{6,5,4,3,2,1,0:T(8,128)(2,1)} %bitcast.91), custom_call_target="tpu_custom_call" | custom-call | tf_op jit(solution)/shard_map/scatter/pallas_call | solution.py:154
  294.8 18.1 %fusion.21 = bf16[2048,1024]{0,1:T(8,128)(2,1)} fusion(bf16[2048,2816]{1,0:T(8,128)(2,1)} %get-tuple-element.37, bf16[2,1024,2816]{2,1,0:T(8,128)(2,1)} %param.13), kind=kOutput, calls=%fused_computation.37 | convolution fusion | flops 11811160064 | bytes 21495808 | tf_op jit(solution)/shard_map/dot_general | solution.py:225
  312.9 19.1 %fusion.20 = (f32[2048]{0:T(1024)S(1)}, bf16[2048,1024]{0,1:T(8,128)(2,1)}) fusion(bf16[2048,1024]{0,1:T(8,128)(2,1)S(1)} %copy-done.4, bf16[2048,1024]{0,1:T(8,128)(2,1)} %fusion.21, bf16[2048,2816]{1,0:T(8,128)(2,1)} %get-tuple-element.36, bf16[2,1024,2816]{2,1,0:T(8,128)(2,1)} %param.14), kind=kOutput, calls=%fused_computation.35 | convolution fusion | flops 11823740928 | bytes 29892608 | tf_op jit(solution)/shard_map/dot_general | solution.py:225
  332.0 6.4 copy.21
  338.5 6.3 fusion.54
  344.7 16.8 %convolution_convert_fusion.4 = bf16[2816,1024]{1,0:T(8,128)(2,1)} fusion(bf16[2048,2816]{1,0:T(8,128)(2,1)} %get-tuple-element.40, bf16[2048,1024]{0,1:T(8,128)(2,1)S(1)} %fusion.54), kind=kOutput, calls=%fused_computation.61 | convolution fusion | flops 11814043648 | bytes 21495808 | tf_op jit(solution)/shard_map/dot_general | solution.py:225
  361.5 17.6 %convolution_convert_fusion = bf16[2048,2816]{1,0:T(8,128)(2,1)} fusion(bf16[2048,1024]{0,1:T(8,128)(2,1)S(1)} %fusion.54, bf16[2,2816,1024]{2,1,0:T(8,128)(2,1)} %param.15), kind=kOutput, calls=%fused_computation.23 | convolution fusion | flops 11816927232 | bytes 21495808 | tf_op jit(solution)/shard_map/dot_general | solution.py:225
  379.1 24.7 %fusion.41 = bf16[1024,2816]{1,0:T(8,128)(2,1)} fusion(f32[2048,2816]{1,0:T(8,128)} %get-tuple-element.41, bf16[2048,2816]{1,0:T(8,128)(2,1)} %convolution_convert_fusion, f32[2048,2816]{1,0:T(8,128)} %fusion.35, bf16[1,2048,1024]{1,2,0:T(8,128)(2,1)S(1)} %copy-done, f32[2048]{0:T(1024)S(1)} %copy-done.15), kind=kOutput, calls=%fused_computation.57 | convolution fusion | flops 11883773952 | bytes 67641344 | tf_op jit(solution)/shard_map/dot_general | solution.py:225
  403.8 22.7 %fusion.44 = bf16[1024,2816]{1,0:T(8,128)(2,1)} fusion(bf16[2048,2816]{1,0:T(8,128)(2,1)} %convolution_convert_fusion, f32[2048,2816]{1,0:T(8,128)} %fusion.35, bf16[1,2048,1024]{1,2,0:T(8,128)(2,1)} %copy.20, f32[2048]{0:T(1024)S(1)} %copy-done.15), kind=kOutput, calls=%fused_computation.58 | convolution fusion | flops 11860705280 | bytes 44572672 | tf_op jit(solution)/shard_map/dot_general | solution.py:225
  426.6 86.4 %scatter.2 = (bf16[88,1024]{1,0:T(8,128)(2,1)}, bf16[32,2816]{1,0:T(8,128)(2,1)}, bf16[32,2816]{1,0:T(8,128)(2,1)}) custom-call(bf16[2,2,2,2,2,88,1024]{6,5,4,3,2,1,0:T(8,128)(2,1)} %bitcast.86, bf16[2,2,2,2,2,32,2816]{6,5,4,3,2,1,0:T(8,128)(2,1)} %bitcast.88, bf16[2,2,2,2,2,32,2816]{6,5,4,3,2,1,0:T(8,128)(2,1)} %bitcast.89), custom_call_target="tpu_custom_call" | custom-call | tf_op jit(solution)/shard_map/scatter/pallas_call | solution.py:154
  519.2 154.0 %gather.1 = (bf16[2,2,2,2,2,2,88,1024]{7,6,5,4,3,2,1,0:T(8,128)(2,1)}, bf16[2,2,2,2,2,2,32,2816]{7,6,5,4,3,2,1,0:T(8,128)(2,1)}, bf16[2,2,2,2,2,2,32,2816]{7,6,5,4,3,2,1,0:T(8,128)(2,1)}) custom-call(bf16[2,88,1024]{2,1,0:T(8,128)(2,1)} %get-tuple-element.33.refs_0_, bf16[2,32,2816]{2,1,0:T(8,128)(2,1)} %get-tuple-element.30.refs_1_, ...), custom_call_target="tpu_custom_call" | custom-call | tf_op jit(solution)/shard_map/gather/pallas_call | solution.py:212
  673.2 11.7 %copy.25 = bf16[2,1024,2816]{2,1,0:T(8,128)(2,1)} copy(bf16[2,1024,2816]{2,1,0:T(8,128)(2,1)} %bitcast.85) | data formatting | bytes 23068672
  684.9 5.8 copy.26
  692.8 4.4 copy.27
  (47 shorter events, 11.9 us)
Async XLA Ops:
  10.2 19.9 %copy-start.14 = (f32[2048]{0:T(1024)}, f32[2048]{0:T(1024)S(1)}, u32[]{:S(2)}) copy-start(f32[2048]{0:T(1024)S(1)} %add_rsqrt_fusion.1) | copy-start | bytes 24580
  79.3 20.2 %copy-start.2 = (bf16[2048,1024]{0,1:T(8,128)(2,1)S(1)}, bf16[2048,1024]{0,1:T(8,128)(2,1)}, u32[]{:S(2)}) copy-start(bf16[2048,1024]{0,1:T(8,128)(2,1)} %get-tuple-element.43) | copy-start | bytes 12582916
  99.5 18.3 %copy-start.5 = (bf16[1,2048,1024]{2,1,0:T(8,128)(2,1)S(1)}, bf16[1,2048,1024]{2,1,0:T(8,128)(2,1)}, u32[]{:S(2)}) copy-start(bf16[1,2048,1024]{2,1,0:T(8,128)(2,1)} %param.12) | copy-start | bytes 12582916
  175.0 18.7 %copy-start.3 = (bf16[2048,1024]{0,1:T(8,128)(2,1)S(1)}, bf16[2048,1024]{0,1:T(8,128)(2,1)}, u32[]{:S(2)}) copy-start(bf16[2048,1024]{0,1:T(8,128)(2,1)} %get-tuple-element.43) | copy-start | bytes 12582916
  175.0 18.7 %copy-start.16 = (bf16[2048,2816]{1,0:T(8,128)(2,1)S(1)}, bf16[2048,2816]{1,0:T(8,128)(2,1)}, u32[]{:S(2)}) copy-start(bf16[2048,2816]{1,0:T(8,128)(2,1)} %get-tuple-element.36) | copy-start | bytes 34603012
  294.8 18.1 %copy-start.4 = (bf16[2048,1024]{0,1:T(8,128)(2,1)S(1)}, bf16[2048,1024]{0,1:T(8,128)(2,1)}, u32[]{:S(2)}) copy-start(bf16[2048,1024]{0,1:T(8,128)(2,1)} %get-tuple-element.43) | copy-start | bytes 12582916
  312.9 25.5 %copy-start.13 = (f32[2048]{0:T(1024)S(1)}, f32[2048]{0:T(1024)}, u32[]{:S(2)}) copy-start(f32[2048]{0:T(1024)} %get-tuple-element.38) | copy-start | bytes 24580
  361.5 17.6 %copy-start = (bf16[1,2048,1024]{1,2,0:T(8,128)(2,1)S(1)}, bf16[1,2048,1024]{1,2,0:T(8,128)(2,1)}, u32[]{:S(2)}) copy-start(bf16[1,2048,1024]{1,2,0:T(8,128)(2,1)} %copy.20) | copy-start | bytes 12582916
  361.5 17.6 %copy-start.15 = (f32[2048]{0:T(1024)S(1)}, f32[2048]{0:T(1024)}, u32[]{:S(2)}) copy-start(f32[2048]{0:T(1024)} %copy-done.14) | copy-start | bytes 24580
  426.6 86.4 %copy-start.6 = (f32[2,88,1024]{2,1,0:T(8,128)S(1)}, f32[2,88,1024]{2,1,0:T(8,128)}, u32[]{:S(2)}) copy-start(f32[2,88,1024]{2,1,0:T(8,128)} %param.21) | copy-start | bytes 2162692
  426.6 86.4 %copy-start.7 = (f32[2,88,1024]{2,1,0:T(8,128)S(1)}, f32[2,88,1024]{2,1,0:T(8,128)}, u32[]{:S(2)}) copy-start(f32[2,88,1024]{2,1,0:T(8,128)} %param.18) | copy-start | bytes 2162692
  426.6 86.4 %copy-start.11 = (bf16[88,1024]{1,0:T(8,128)(2,1)S(1)}, bf16[88,1024]{1,0:T(8,128)(2,1)}, u32[]{:S(2)}) copy-start(bf16[88,1024]{1,0:T(8,128)(2,1)} %get-tuple-element.19) | copy-start | bytes 540676
  426.6 88.9 %copy-start.8 = (f32[2,32,2816]{2,1,0:T(8,128)S(1)}, f32[2,32,2816]{2,1,0:T(8,128)}, u32[]{:S(2)}) copy-start(f32[2,32,2816]{2,1,0:T(8,128)} %param.19) | copy-start | bytes 2162692
  426.6 88.9 %copy-start.9 = (f32[2,32,2816]{2,1,0:T(8,128)S(1)}, f32[2,32,2816]{2,1,0:T(8,128)}, u32[]{:S(2)}) copy-start(f32[2,32,2816]{2,1,0:T(8,128)} %param.16) | copy-start | bytes 2162692
  426.6 88.9 %copy-start.10 = (f32[2,32,2816]{2,1,0:T(8,128)S(1)}, f32[2,32,2816]{2,1,0:T(8,128)}, u32[]{:S(2)}) copy-start(f32[2,32,2816]{2,1,0:T(8,128)} %param.20) | copy-start | bytes 2162692
  426.6 88.9 %copy-start.12 = (bf16[32,2816]{1,0:T(8,128)(2,1)S(1)}, bf16[32,2816]{1,0:T(8,128)(2,1)}, u32[]{:S(2)}) copy-start(bf16[32,2816]{1,0:T(8,128)(2,1)} %get-tuple-element.21) | copy-start | bytes 540676
  673.2 11.7 %copy-start.1 = (bf16[2,2,2,2,2,2,32,2816]{7,6,5,4,3,2,1,0:T(8,128)(2,1)S(1)}, bf16[2,2,2,2,2,2,32,2816]{7,6,5,4,3,2,1,0:T(8,128)(2,1)}, u32[]{:S(2)}) copy-start(bf16[2,2,2,2,2,2,32,2816]{7,6,5,4,3,2,1,0:T(8,128)(2,1)} %get-tuple-element.25) | copy-start | bytes 34603012
  673.2 17.6 %slice-start = ((s8[11534336]{0:T(1024)(128)(4,1)}), s8[4194304]{0:T(1024)(128)(4,1)S(1)}, s32[]{:S(2)}) async-start(s8[11534336]{0:T(1024)(128)(4,1)} %bitcast.81), calls=%async_computation | async-start | bytes 8388608
  673.2 18.2 %slice-start.1 = ((s8[11534336]{0:T(1024)(128)(4,1)}), s8[4194304]{0:T(1024)(128)(4,1)S(1)}, s32[]{:S(2)}) async-start(s8[11534336]{0:T(1024)(128)(4,1)} %bitcast.81), calls=%async_computation.1 | async-start | bytes 8388608
  684.9 7.8 %slice-start.2 = ((s8[11534336]{0:T(1024)(128)(4,1)}), s8[3145728]{0:T(1024)(128)(4,1)S(1)}, s32[]{:S(2)}) async-start(s8[11534336]{0:T(1024)(128)(4,1)} %bitcast.81), calls=%async_computation.2 | async-start | bytes 6291456

commit v2 on v1

v2 whole, which is shorter than its diff:
```python
import functools

import jax
import jax.numpy as jnp
from jax import lax
from jax.experimental import pallas as pl
from jax.experimental.pallas import tpu as pltpu
from jax.sharding import PartitionSpec as P

F32, BF16 = jnp.float32, jnp.bfloat16
AXES = "dp"


DIMS = {"x": 16, "y": 8, "b": 4, "a": 2, "c": 1}
LEAD = "xyba"
PARTS = {
    2816: ((0, 1152, "xyab"), (1152, 2304, "yxab"), (2304, 2816, "abxy")),
    1024: ((0, 384, "xyab"), (384, 768, "yxab"), (768, 1024, "abyx")),
}
STEP = {32: 384, 88: 128}


def place():
    me = lax.axis_index(AXES)
    own = {d: (me // s) % 2 for d, s in DIMS.items()}
    peer = {d: me + (1 - 2 * own[d]) * s for d, s in DIMS.items()}
    return own, peer


def greet(peer):
    barrier = pltpu.get_barrier_semaphore()
    for d in DIMS:
        pl.semaphore_signal(barrier, inc=1, device_id={AXES: peer[d]}, device_id_type=pl.DeviceIdType.MESH)
    pl.semaphore_wait(barrier, len(DIMS))


def remote(src, dst, sems, n, target):
    return pltpu.make_async_remote_copy(
        src_ref=src, dst_ref=dst, send_sem=sems[0].at[n], recv_sem=sems[1].at[n], device_id={AXES: target}, device_id_type=pl.DeviceIdType.MESH
    )


def steps_of(lo, hi, rows):
    step = STEP[rows]
    return [(at, min(step, hi - at)) for at in range(lo, hi, step)]


def in_turn(steps, count):
    return sorted(((k, i) for k in range(steps) for i in range(count)), key=lambda at: 1.5 * at[0] + at[1])


class Scatter:
    def __init__(self, grad, held, came, later, out, sems, local, first, own, peer):
        self.grad, self.held, self.came, self.later, self.out = grad, held, came, later, out
        self.own, self.peer = own, peer
        self.rows, self.cols = grad.shape[-2:]
        self.parts = PARTS[self.cols]
        self.copies, n = {}, first
        for p, (lo, hi, order) in enumerate(self.parts):
            for half in range(2):
                at = tuple((1 - own[d] if half == 0 else own[d]) if d == order[0] else slice(None) for d in LEAD)
                here = at + (slice(None), pl.ds(lo, hi - lo))
                mine, theirs = at + (own["c"], slice(None), pl.ds(lo, hi - lo)), at + (1 - own["c"], slice(None), pl.ds(lo, hi - lo))
                self.copies["c", p, half] = remote(grad.at[theirs], came.at[here], sems, n, peer["c"])
                self.copies["own", p, half] = pltpu.make_async_copy(grad.at[mine], held.at[here], local.at[n])
                n += 1
            for k, d in enumerate(order):
                at = tuple(own[e] if e in order[:k] else 1 - own[e] if e == d else slice(None) for e in LEAD)
                self.copies[k, p] = remote(held.at[at + (slice(None), pl.ds(lo, hi - lo))], later[p][k], sems, n, peer[d])
                n += 1
        self.used = n - first

    def begin(self, half):
        for p in range(len(self.parts)):
            self.copies["c", p, half].start()
            self.copies["own", p, half].start()

    def add(self, p, k):
        lo, hi, order = self.parts[p]
        free = order[k + 1 :]

        def block(i, _):
            at = {}
            for n, e in enumerate(order):
                at[e] = self.own[e] if n < k else 1 - self.own[e] if n == k else (i // 2 ** (len(order) - 1 - n)) % 2
            lead = tuple(at[e] for e in LEAD)
            for c, size in steps_of(lo, hi, self.rows):
                here = lead + (slice(None), pl.ds(c, size))
                total = self.held[here].astype(F32) + self.came[here].astype(F32)
                for j in range(min(k, len(order))):
                    inner = tuple(at[e] for e in LEAD if e in order[j + 1 :])
                    total = total + self.later[p][j][inner + (slice(None), pl.ds(c - lo, size))].astype(F32)
                if k < len(order):
                    self.held[here] = total.astype(BF16)
                else:
                    self.out[:, pl.ds(c, size)] = total.astype(BF16)
            return 0

        if len(free) == 0:
            block(0, 0)
        else:
            lax.fori_loop(0, 2 ** len(free), block, 0)

    def send(self, p, k):
        if k == 0:
            self.copies["c", p, 0].wait_recv()
            self.copies["own", p, 0].wait()
        else:
            if k == 1:
                self.copies["c", p, 1].wait_recv()
                self.copies["own", p, 1].wait()
            self.copies[k - 1, p].wait_recv()
        self.add(p, k)
        if k < 4:
            self.copies[k, p].start()

    def finish(self):
        for name, copy in self.copies.items():
            if name[0] != "own":
                copy.wait_send()


def copies_of(cols):
    return len(PARTS[cols]) * 6


def later_shapes(rows, cols):
    return [[pltpu.VMEM((2,) * (3 - k) + (rows, hi - lo), BF16) for k in range(4)] for lo, hi, _ in PARTS[cols]]


class Gather:
    def __init__(self, block, out, sems, local, first, own, peer):
        rows, cols = block.shape
        every = slice(None)
        self.parts = PARTS[cols]
        self.keep = pltpu.make_async_copy(block, out.at[tuple(own[e] for e in LEAD) + (own["c"],)], local.at[first])
        self.copies, n = {}, first
        for p, (lo, hi, order) in enumerate(self.parts):
            at_cols = (every, pl.ds(lo, hi - lo))
            for k, d in enumerate(order[::-1] + "c"):
                got = order[::-1][:k]
                at = tuple(every if e in got else own[e] for e in LEAD) + (own["c"],) + at_cols
                self.copies[k, p] = remote(block.at[at_cols] if k == 0 else out.at[at], out.at[at], sems, n, peer[d])
                n += 1
        self.used = n - first

    def begin(self, half):
        if half == 0:
            self.keep.start()

    def send(self, p, k):
        if k == 1 and p == 0:
            self.keep.wait()
        if k:
            self.copies[k - 1, p].wait_recv()
        self.copies[k, p].start()

    def finish(self):
        for (k, _), copy in self.copies.items():
            if k == 4:
                copy.wait_recv()
            copy.wait_send()


def host(name, body, steps, ins, outs, args, scratch=(), grads=(), blocks=(), collective_id=None, flops=0):
    grads = [g.reshape((2,) * 5 + (g.shape[0] // 32, g.shape[1])) for g in grads]
    shapes = [g.shape[5:] for g in grads]
    counts = [len(ins), len(grads), len(blocks), len(outs), len(grads), len(blocks), len(scratch)]
    total = sum(copies_of(s[1]) for s in shapes) + sum(5 * len(PARTS[b.shape[1]]) for b in blocks)
    anywhere, units_count = pl.BlockSpec(memory_space=pl.ANY), len(grads) + len(blocks)

    def kernel(*refs):
        refs, groups = list(refs), []
        for n in counts:
            groups.append(refs[:n])
            refs = refs[n:]
        mine, grad_refs, block_refs, results, sums, gathered, own_scratch = groups
        step = pl.program_id(0)
        if units_count:
            held, came, later, sems, local = refs
            own, peer = place()
            work, n = [], 0
            for i in range(len(grads)):
                work.append(Scatter(grad_refs[i], held[i], came[i], later[i], sums[i], sems, local, n, own, peer))
                n += work[-1].used
            for i in range(len(blocks)):
                work.append(Gather(block_refs[i], gathered[i], sems, local, n, own, peer))
                n += work[-1].used
            turns = in_turn(5, units_count)

            def begin():
                greet(peer)
                for half in range(2):
                    for w in work:
                        w.begin(half)

            def at(which):
                for k, i in which:
                    for p in range(len(work[i].parts)):
                        work[i].send(p, k)

            def finish():
                for w in work:
                    w.finish()

            if steps == 1:
                begin()
                at(turns)
                finish()
            else:
                pl.when(step == 0)(begin)
                when = {}
                for n, turn in enumerate(turns):
                    when.setdefault(1 + n * (steps - 1) // len(turns), []).append(turn)
                for n, which in when.items():
                    pl.when(step == n)(functools.partial(at, which))
        if body is not None:
            body(step, *mine, *results, *own_scratch)
        if units_count and steps > 1:
            pl.when(step == steps - 1)(finish)

    comm_scratch = []
    if units_count:
        comm_scratch = [
            [pltpu.VMEM((2, 2, 2, 2) + s, BF16) for s in shapes],
            [pltpu.VMEM((2, 2, 2, 2) + s, BF16) for s in shapes],
            [later_shapes(*s) for s in shapes],
            [pltpu.SemaphoreType.DMA((total,)), pltpu.SemaphoreType.DMA((total,))],
            pltpu.SemaphoreType.DMA((total,)),
        ]
    params = dict(collective_id=collective_id, has_side_effects=True) if units_count else {}
    whole = lambda s: pl.BlockSpec(s, lambda i: (0, 0))
    results = pl.pallas_call(
        kernel,
        name=name,
        grid=(steps,),
        in_specs=list(ins) + [anywhere] * units_count,
        out_specs=[o[0] for o in outs] + [whole(s) for s in shapes] + [anywhere] * len(blocks),
        out_shape=[jax.ShapeDtypeStruct(*o[1:]) for o in outs]
        + [jax.ShapeDtypeStruct(s, BF16) for s in shapes]
        + [jax.ShapeDtypeStruct((2,) * 5 + b.shape, BF16) for b in blocks],
        scratch_shapes=list(scratch) + comm_scratch,
        compiler_params=pltpu.CompilerParams(vmem_limit_bytes=62 * 2**20, dimension_semantics=("arbitrary",), **params),
        cost_estimate=pl.CostEstimate(flops=flops + 10**9, bytes_accessed=60 * 2**20, transcendentals=0),
    )(*args, *grads, *blocks)
    a, b = len(outs), len(outs) + len(grads)
    return results[:a], results[a:b], [r.reshape(-1, r.shape[-1]) for r in results[b:]]


def dot(a, b, contract):
    return lax.dot_general(a, b, ((contract[:1], contract[1:]), ((), ())), preferred_element_type=F32)


def norm_scale(h):
    wide = h.astype(F32)
    return lax.rsqrt(jnp.mean(wide**2, -1, keepdims=True) + 1e-6)


def adamw(w, m, v, g):
    m = 0.9 * m + 0.1 * g
    v = 0.95 * v + 0.05 * g * g
    step = m * lax.rsqrt(v + 1e-8) + 0.1 * w
    return (w - 0.02 * step).astype(BF16), m, v


def silu_parts(gate):
    s = 0.5 * jnp.tanh(0.5 * gate) + 0.5
    y = gate * s
    return y, s + y * (1 - s)


TM = 128
CHUNKS = [(at, min(512, 2816 - at)) for at in range(0, 2816, 512)]
HALVES = [(0, 512), (512, 512)]


def fetch(refs, bufs, sems):
    return [pltpu.make_async_copy(r, b, sems.at[n]) for n, (r, b) in enumerate(zip(refs, bufs))]


def scale_of(h):
    wide = h.astype(F32)
    return wide, lax.rsqrt(jnp.mean(wide * wide, -1, keepdims=True) + 1e-6)


def forth_kernel(x, dy, wg, wu, wd, a0o, g0o, u0o, p0o, h1o, a1o, p1o, dg1o, du1o, wg0, wu0, wd0, wg1, wu1, wd1, sems):
    bufs = (wg0, wu0, wd0, wd1, wg1, wu1)
    copies = fetch([wg.at[0], wu.at[0], wd.at[0], wd.at[1], wg.at[1], wu.at[1]], bufs, sems)
    first = pl.program_id(0) == 0

    def need(*which):
        @pl.when(first)
        def _():
            for n in which:
                copies[n].wait()

    @pl.when(first)
    def _():
        for copy in copies:
            copy.start()

    wide, r = scale_of(x[...])
    a = (wide * r).astype(BF16)
    a0o[...] = a
    need(0, 1)
    for at, size in CHUNKS:
        cols = pl.ds(at, size)
        g = dot(a, wg0[:, cols], (1, 0))
        u = dot(a, wu0[:, cols], (1, 0))
        g0o[:, cols] = g
        u0o[:, cols] = u
        p0o[:, cols] = (silu_parts(g)[0] * u).astype(BF16)
    need(2)
    for at, size in HALVES:
        cols = pl.ds(at, size)
        h1o[:, cols] = x[:, cols] + dot(p0o[...], wd0[:, cols], (1, 0)).astype(BF16)
    wide, r = scale_of(h1o[...])
    a = (wide * r).astype(BF16)
    a1o[...] = a
    need(3, 4, 5)
    d = dy[...]
    for at, size in CHUNKS:
        cols = pl.ds(at, size)
        g = dot(a, wg1[:, cols], (1, 0))
        u = dot(a, wu1[:, cols], (1, 0))
        dp = dot(d, wd1[cols, :], (1, 1)).astype(BF16).astype(F32)
        s, ds = silu_parts(g)
        p1o[:, cols] = (s * u).astype(BF16)
        dg1o[:, cols] = (dp * u * ds).astype(BF16)
        du1o[:, cols] = (dp * s).astype(BF16)


def forth(x, dy, wg, wu, wd):
    tokens, d = x.shape
    ff = wg.shape[2]
    spec = lambda n: pl.BlockSpec((TM, n), lambda i: (i, 0))
    outs = [(d, BF16), (ff, F32), (ff, F32), (ff, BF16), (d, BF16), (d, BF16), (ff, BF16), (ff, BF16), (ff, BF16)]
    return pl.pallas_call(
        forth_kernel,
        name="forth",
        grid=(tokens // TM,),
        in_specs=[spec(d), spec(d)] + [pl.BlockSpec(memory_space=pl.ANY)] * 3,
        out_specs=[spec(n) for n, _ in outs],
        out_shape=[jax.ShapeDtypeStruct((tokens, n), t) for n, t in outs],
        scratch_shapes=[pltpu.VMEM(s, BF16) for s in ((d, ff), (d, ff), (ff, d)) * 2] + [pltpu.SemaphoreType.DMA((6,))],
        compiler_params=pltpu.CompilerParams(vmem_limit_bytes=62 * 2**20, dimension_semantics=("arbitrary",)),
        cost_estimate=pl.CostEstimate(flops=12 * tokens * d * ff, bytes_accessed=180 * 2**20, transcendentals=2 * tokens * ff),
    )(x, dy, wg, wu, wd)


def back_body(step, dg1, du1, dy, h1, g0, u0, wg, wu, wd, dh1o, dg0o, du0o, wg1, wu1, wd0, sems):
    copies = fetch([wg.at[1], wu.at[1], wd.at[0]], (wg1, wu1, wd0), sems)

    @pl.when(step == 0)
    def _():
        for copy in copies:
            copy.start()
        for copy in copies:
            copy.wait()

    by_gate = dot(dg1[...], wg1[...], (1, 1)).astype(BF16)
    by_up = dot(du1[...], wu1[...], (1, 1)).astype(BF16)
    da = (by_gate + by_up).astype(F32)
    wide, r = scale_of(h1[...])
    inner = jnp.mean(da * wide, -1, keepdims=True)
    dh1o[...] = dy[...] + (da * r - wide * (r * r * r) * inner).astype(BF16)
    d = dh1o[...]
    for at, size in CHUNKS:
        cols = pl.ds(at, size)
        dp = dot(d, wd0[cols, :], (1, 1)).astype(BF16).astype(F32)
        s, ds = silu_parts(g0[:, cols])
        dg0o[:, cols] = (dp * u0[:, cols] * ds).astype(BF16)
        du0o[:, cols] = (dp * s).astype(BF16)


def back(dg1, du1, dy, h1, g0, u0, wg, wu, wd, **beside):
    tokens, d = dy.shape
    ff = wg.shape[2]
    tm = 256
    spec = lambda n: pl.BlockSpec((tm, n), lambda i: (i, 0))
    return host(
        "back",
        back_body,
        tokens // tm,
        [spec(n) for n in (ff, ff, d, d, ff, ff)] + [pl.BlockSpec(memory_space=pl.ANY)] * 3,
        [(spec(n), (tokens, n), BF16) for n in (d, ff, ff)],
        (dg1, du1, dy, h1, g0, u0, wg, wu, wd),
        [pltpu.VMEM(s, BF16) for s in ((d, ff), (d, ff), (ff, d))] + [pltpu.SemaphoreType.DMA((3,))],
        flops=6 * tokens * d * ff,
        **beside,
    )


def outers(p, d, a, wide, **beside):
    tokens, tile = a.shape[0], 256
    ff, dim = wide[0].shape[1], a.shape[1]
    tiles = ff // tile
    downs = tiles if p is not None else 0
    steps = downs + tiles * len(wide)
    ins, outs, args, scratch = [], [], [], []
    if p is not None:
        ins += [pl.BlockSpec((tokens, tile), lambda i: (0, jnp.minimum(i, tiles - 1))), pl.BlockSpec((tokens, dim), lambda i: (0, 0))]
        outs.append((pl.BlockSpec((tile, dim), lambda i: (jnp.minimum(i, tiles - 1), 0)), (ff, dim), BF16))
        args += [p, d]
    if wide:
        ins.append(pl.BlockSpec((tokens, dim), lambda i: (0, 0)))
        args.append(a)
        scratch.append(pltpu.VMEM((dim, tokens), BF16))

    def column(first):
        return lambda i: (0, jnp.clip(i - first, 0, tiles - 1))

    for n, w in enumerate(wide):
        ins.append(pl.BlockSpec((tokens, tile), column(downs + n * tiles)))
        outs.append((pl.BlockSpec((dim, tile), column(downs + n * tiles)), (dim, ff), BF16))
        args.append(w)

    def work(step, *refs):
        refs = list(refs)
        if p is not None:
            p_ref, d_ref = refs[:2]
            refs = refs[2:]
        a_ref, w_refs, o_refs, turned = refs[0], refs[1 : 1 + len(wide)], refs[1 + len(wide) : -1], refs[-1]

        if p is not None:

            @pl.when(step < downs)
            def _():
                for at, size in HALVES:
                    o_refs[0][:, pl.ds(at, size)] = dot(p_ref[...], d_ref[:, pl.ds(at, size)], (0, 0)).astype(BF16)

        @pl.when(step == downs)
        def _():
            for at in range(0, tokens, 512):
                turned[:, pl.ds(at, 512)] = a_ref[pl.ds(at, 512), :].T

        for n in range(len(wide)):
            first, w_ref, o_ref = downs + n * tiles, w_refs[n], o_refs[n - len(wide)]

            @pl.when((step >= first) & (step < first + tiles))
            def _():
                o_ref[...] = dot(turned[...], w_ref[...], (1, 0)).astype(BF16)

    return host("outers", work, steps, ins, outs, args, scratch, flops=2 * tokens * tile * dim * steps, **beside)


def outer(a, b, tile=256):
    tokens, m = a.shape
    n = b.shape[1]

    def work(step, a_ref, b_ref, o):
        for at, size in HALVES:
            o[:, pl.ds(at, size)] = dot(a_ref[...], b_ref[:, pl.ds(at, size)], (0, 0)).astype(BF16)

    ins = [pl.BlockSpec((tokens, tile), lambda i: (0, i)), pl.BlockSpec((tokens, n), lambda i: (0, 0))]
    outs = [(pl.BlockSpec((tile, n), lambda i: (i, 0)), (m, n), BF16)]
    return host("outer", work, m // tile, ins, outs, (a, b), flops=2 * tokens * m * n)[0][0]


def body(x, dy, wg, wu, wd, mg, mu, md, vg, vu, vd):
    x, dy = x[0], dy[0]
    i = lax.axis_index(AXES)

    def update(layer, w, m, v, g):
        rows = m.shape[1]
        mine = lax.dynamic_slice_in_dim(w[layer], i * rows, rows, 0).astype(F32)
        return adamw(mine, m[layer], v[layer], g.astype(F32))

    a0, g0, u0, p0, h1, a1, p1, dg1, du1 = forth(x, dy, wg, wu, wd)
    dwd1 = outer(p1, dy)
    (dwg1, dwu1), (sd1,), _ = outers(None, None, a1, [dg1, du1], grads=[dwd1], collective_id=0)
    nd1 = update(1, wd, md, vd, sd1)
    (dh1, dg0, du0), (sg1, su1), _ = back(dg1, du1, dy, h1, g0, u0, wg, wu, wd, grads=[dwg1, dwu1], collective_id=1)
    ng1 = update(1, wg, mg, vg, sg1)
    nu1 = update(1, wu, mu, vu, su1)
    (dwd0, dwg0, dwu0), _, (fd1, fg1) = outers(p0, dh1, a0, [dg0, du0], blocks=[nd1[0], ng1[0]], collective_id=2)
    _, (sd0, sg0, su0), (fu1,) = host("ends", None, 1, [], [], (), grads=[dwd0, dwg0, dwu0], blocks=[nu1[0]], collective_id=3)
    nd0, ng0, nu0 = update(0, wd, md, vd, sd0), update(0, wg, mg, vg, sg0), update(0, wu, mu, vu, su0)
    _, _, (fd0, fg0, fu0) = host("last", None, 1, [], [], (), blocks=[nd0[0], ng0[0], nu0[0]], collective_id=4)
    stacked = [jnp.stack(pair) for pair in ((fg0, fg1), (fu0, fu1), (fd0, fd1))]
    for which in (1, 2):
        stacked += [jnp.stack([a[which], b[which]]) for a, b in ((ng0, ng1), (nu0, nu1), (nd0, nd1))]
    return tuple(stacked)


def solution(mesh):
    whole, seq, part = P(None, None, None), P(("rep", "dp"), None, None), P(None, "dp", None)
    outw, outm = P("rep", None, None), P("rep", "dp", None)
    return jax.shard_map(body, mesh=mesh, in_specs=(seq, seq) + (whole,) * 3 + (part,) * 6, out_specs=(outw,) * 3 + (outm,) * 6, check_vma=False)
```

time: 704 us -> 637 us (0.905)
  matrix products: 316 us -> 0 us
  Pallas kernels: 327 us -> 566 us
  other arithmetic: 16.1 us -> 39.4 us
    dot_general x15 -> x0, matrix products: 316 us -> none  [dot(): lax.dot_general(a, b, ((contract[:1], contract[1:]), ((), ())), preferred...]
    pallas_call x3 -> x7, Pallas kernels: 327 us -> 566 us  [the longest x6 453 us: host(): pl.pallas_call(kernel, name=name, grid=(steps,), in_specs=list(ins) + [an...]
    another operation x0 -> x14, other arithmetic: none -> 39.4 us  [the longest x3 22.6 us: body(): stacked = [jnp.stack(pair) for pair in ((fg0, fg1), (fu0, fu1), (fd0, fd1))]]
    unnamed x45 -> x34, local copies, waits for them, and re-layouts: 37 us -> 1.41 us
    slice x0 -> x3, local copies, waits for them, and re-layouts: none -> 29.4 us  [update(): mine = lax.dynamic_slice_in_dim(w[layer], i * rows, rows, 0).astype(F32)]
where the time goes in v2:
time: 637 us
  Pallas kernels  566 us (89%)
  other arithmetic  39.4 us (6%)
  local copies, waits for them, and re-layouts  30.8 us (5%)
    pallas_call x6, Pallas kernels, host(): pl.pallas_call(kernel, name=name, grid=(steps,), in_specs=list(ins) + [an...  453 us
    pallas_call x1, Pallas kernels, forth(): pl.pallas_call(forth_kernel, name='forth', grid=(tokens // TM,), in_specs...  112 us
    slice x3, local copies, waits for them, and re-layouts, update(): mine = lax.dynamic_slice_in_dim(w[layer], i * rows, rows, 0).astype(F32)  29.4 us
    another operation x3, other arithmetic, body(): stacked = [jnp.stack(pair) for pair in ((fg0, fg1), (fu0, fu1), (fd0, fd1))]  22.6 us
    another operation x11, other arithmetic, body(): jnp.stack([a[which], b[which]])  16.8 us

profile of v2, /device:TPU:0, one launch (start us, length us, event | category | flops | bytes accessed | tf_op | source)
XLA Modules:
  0.0 636.6 jit_solution(5860205480689637057)
XLA Ops:
  0.6 112.4 %forth.1 = (bf16[2048,1024]{1,0:T(8,128)(2,1)}, f32[2048,2816]{1,0:T(8,128)}, f32[2048,2816]{1,0:T(8,128)}, bf16[2048,2816]{1,0:T(8,128)(2,1)}, bf16[2048,1024]{...) custom-call(bf16[2048,1024]{1,0:T(8,128)(2,1)} %bitcast.143, ...), custom_call_target="tpu_custom_call" | custom-call | flops 70866960384 | bytes 188743680 | tf_op jit(solution)/shard_map/forth/pallas_call | solution.py:338
  113.1 18.2 %outer.1 = bf16[2816,1024]{1,0:T(8,128)(2,1)} custom-call(bf16[2048,2816]{1,0:T(8,128)(2,1)} %get-tuple-element.45.refs_0_, bf16[2048,1024]{1,0:T(8,128)(2,1)} %bitcast.145), custom_call_target="tpu_custom_call" | custom-call | flops 12811159552 | bytes 62914560 | tf_op jit(solution)/shard_map/outer/pallas_call | solution.py:233
  131.3 56.7 %outers.2 = (bf16[1024,2816]{1,0:T(8,128)(2,1)}, bf16[1024,2816]{1,0:T(8,128)(2,1)}, bf16[88,1024]{1,0:T(8,128)(2,1)}) custom-call(bf16[2048,1024]{1,0:T(8,128)(2,1)} %get-tuple-element.44.refs_0_, bf16[2048,2816]{1,0:T(8,128)(2,1)} %get-tuple-element.39.refs_1_.refs_0_, bf16[2048,2816]{1,0:T(8,128)(2,1)} %get-tuple-element.40.refs_2_.refs_1_, ...), custom_call_target="tpu_custom_call" | custom-call | flops 24622319616 | bytes 62914560 | tf_op jit(solution)/shard_map/outers/pallas_call | solution.py:233
  188.0 94.5 %back.1 = (bf16[2048,1024]{1,0:T(8,128)(2,1)}, bf16[2048,2816]{1,0:T(8,128)(2,1)}, bf16[2048,2816]{1,0:T(8,128)(2,1)}, bf16[32,2816]{1,0:T(8,128)(2,1)}, bf16[32,2816]{1,0:T(8,128)(2,1)}) custom-call(bf16[2048,2816]{1,0:T(8,128)(2,1)} %get-tuple-element.39.refs_1_.refs_0_, bf16[2048,2816]{1,0:T(8,128)(2,1)} %get-tuple-element.40.refs_2_.refs_1_, ...), custom_call_target="tpu_custom_call" | custom-call | flops 36433481728 | bytes 62914560 | tf_op jit(solution)/shard_map/back/pallas_call | solution.py:233
  282.6 9.5 %fusion.42 = (bf16[1,1024,2816]{2,1,0:T(8,128)(2,1)}, bf16[1,1024,2816]{2,1,0:T(8,128)(2,1)}) fusion(bf16[2,1024,2816]{2,1,0:T(8,128)(2,1)} %refs_7_.1), kind=kLoop, calls=%fused_computation.75 | loop fusion | bytes 23068672 | tf_op jit(solution)/shard_map/slice | solution.py:466
  292.1 9.6 %fusion.43 = (bf16[1,1024,2816]{2,1,0:T(8,128)(2,1)}, bf16[1,1024,2816]{2,1,0:T(8,128)(2,1)}) fusion(bf16[2,1024,2816]{2,1,0:T(8,128)(2,1)} %refs_6_.1), kind=kLoop, calls=%fused_computation.76 | loop fusion | bytes 23068672 | tf_op jit(solution)/shard_map/slice | solution.py:466
  301.7 2.4 fusion.38
  304.1 10.3 %fusion.44 = (bf16[1,2816,1024]{2,1,0:T(8,128)(2,1)}, bf16[1,2816,1024]{2,1,0:T(8,128)(2,1)}) fusion(bf16[2,2816,1024]{2,1,0:T(8,128)(2,1)} %refs_8_.1), kind=kLoop, calls=%fused_computation.77 | loop fusion | bytes 23068672 | tf_op jit(solution)/shard_map/slice | solution.py:466
  314.4 1.9 fusion.41
  316.3 77.0 %outers.3 = (bf16[2816,1024]{1,0:T(8,128)(2,1)}, bf16[1024,2816]{1,0:T(8,128)(2,1)}, bf16[1024,2816]{1,0:T(8,128)(2,1)}, bf16[2,2,2,2,2,88,1024]{6,5,4,3,2,1,0:T...) custom-call(bf16[2048,2816]{1,0:T(8,128)(2,1)} %get-tuple-element.38.refs_0_, bf16[2048,1024]{1,0:T(8,128)(2,1)} %get-tuple-element.48.refs_1_, ...), custom_call_target="tpu_custom_call" | custom-call | flops 36433481728 | bytes 62914560 | tf_op jit(solution)/shard_map/outers/pallas_call | solution.py:233
  393.3 108.6 %ends.1 = (bf16[88,1024]{1,0:T(8,128)(2,1)}, bf16[32,2816]{1,0:T(8,128)(2,1)}, bf16[32,2816]{1,0:T(8,128)(2,1)}, bf16[2,2,2,2,2,32,2816]{6,5,4,3,2,1,0:T(8,128)(2,1)}) custom-call(bf16[2,2,2,2,2,88,1024]{6,5,4,3,2,1,0:T(8,128)(2,1)} %bitcast.128, bf16[2,2,2,2,2,32,2816]{6,5,4,3,2,1,0:T(8,128)(2,1)} %bitcast.129, ...), custom_call_target="tpu_custom_call" | custom-call | flops 1000000000 | bytes 62914560 | tf_op jit(solution)/shard_map/ends/pallas_call | solution.py:233
  501.9 2.2 fusion.40
  504.1 1.9 pad_maximum_fusion.8
  506.0 2.1 fusion.36
  508.1 0.9 pad_maximum_fusion.7
  509.0 1.8 fusion.37
  511.7 0.9 pad_maximum_fusion.5
  512.7 0.9 pad_maximum_fusion.4
  513.6 0.9 pad_maximum_fusion.3
  514.5 98.1 %last.1 = (bf16[2,2,2,2,2,88,1024]{6,5,4,3,2,1,0:T(8,128)(2,1)}, bf16[2,2,2,2,2,32,2816]{6,5,4,3,2,1,0:T(8,128)(2,1)}, bf16[2,2,2,2,2,32,2816]{6,5,4,3,2,1,0:T(8,128)(2,1)}) custom-call(bf16[88,1024]{1,0:T(8,128)(2,1)} %get-tuple-element.74.refs_0_, bf16[32,2816]{1,0:T(8,128)(2,1)} %get-tuple-element.86.refs_1_, bf16[32,2816]{1,0:T(8,128)(2,1)} %get-tuple-element.80.refs_2_), custom_call_target="tpu_custom_call" | custom-call | flops 1000000000 | bytes 62914560 | tf_op jit(solution)/shard_map/last/pallas_call | solution.py:233
  612.6 11.7 %pad_maximum_fusion.2 = bf16[2,2816,1024]{2,1,0:T(8,128)(2,1)} fusion(bf16[1,2816,1024]{2,1,0:T(8,128)(2,1)} %bitcast.134, bf16[1,2816,1024]{2,1,0:T(8,128)(2,1)} %bitcast.142), kind=kLoop, calls=%fused_computation.2 | loop fusion | flops 5767168 | bytes 23068672 | tf_op jit(solution)/shard_map/stack | solution.py:480
  624.3 5.9 pad_maximum_fusion.1
  630.4 1.1 slice-done.5
  631.6 5.0 pad_maximum_fusion
  (37 shorter events, 1.2 us)
Async XLA Ops:
  292.1 9.6 %copy-start.3 = (f32[2,32,2816]{2,1,0:T(8,128)S(1)}, f32[2,32,2816]{2,1,0:T(8,128)}, u32[]{:S(2)}) copy-start(f32[2,32,2816]{2,1,0:T(8,128)} %param.20) | copy-start | bytes 2162692
  292.1 9.6 %copy-start.4 = (f32[2,32,2816]{2,1,0:T(8,128)S(1)}, f32[2,32,2816]{2,1,0:T(8,128)}, u32[]{:S(2)}) copy-start(f32[2,32,2816]{2,1,0:T(8,128)} %param.17) | copy-start | bytes 2162692
  292.1 9.6 %copy-start.7 = (bf16[32,2816]{1,0:T(8,128)(2,1)S(1)}, bf16[32,2816]{1,0:T(8,128)(2,1)}, u32[]{:S(2)}) copy-start(bf16[32,2816]{1,0:T(8,128)(2,1)} %get-tuple-element.53) | copy-start | bytes 540676
  292.1 9.6 %copy-start.8 = (bf16[32,2816]{1,0:T(8,128)(2,1)S(1)}, bf16[32,2816]{1,0:T(8,128)(2,1)}, u32[]{:S(2)}) copy-start(bf16[32,2816]{1,0:T(8,128)(2,1)} %get-tuple-element.57) | copy-start | bytes 540676
  304.1 10.3 %copy-start.1 = (f32[2,88,1024]{2,1,0:T(8,128)S(1)}, f32[2,88,1024]{2,1,0:T(8,128)}, u32[]{:S(2)}) copy-start(f32[2,88,1024]{2,1,0:T(8,128)} %param.21) | copy-start | bytes 2162692
  304.1 10.3 %copy-start.2 = (f32[2,88,1024]{2,1,0:T(8,128)S(1)}, f32[2,88,1024]{2,1,0:T(8,128)}, u32[]{:S(2)}) copy-start(f32[2,88,1024]{2,1,0:T(8,128)} %param.18) | copy-start | bytes 2162692
  304.1 10.3 %copy-start.9 = (bf16[88,1024]{1,0:T(8,128)(2,1)S(1)}, bf16[88,1024]{1,0:T(8,128)(2,1)}, u32[]{:S(2)}) copy-start(bf16[88,1024]{1,0:T(8,128)(2,1)} %get-tuple-element.52) | copy-start | bytes 540676
  501.8 7.2 %copy-start.5 = (f32[2,32,2816]{2,1,0:T(8,128)S(1)}, f32[2,32,2816]{2,1,0:T(8,128)}, u32[]{:S(2)}) copy-start(f32[2,32,2816]{2,1,0:T(8,128)} %param.16) | copy-start | bytes 2162692
  501.9 7.2 %copy-start.6 = (f32[2,32,2816]{2,1,0:T(8,128)S(1)}, f32[2,32,2816]{2,1,0:T(8,128)}, u32[]{:S(2)}) copy-start(f32[2,32,2816]{2,1,0:T(8,128)} %param.19) | copy-start | bytes 2162692
  501.9 7.2 %copy-start.10 = (bf16[32,2816]{1,0:T(8,128)(2,1)S(1)}, bf16[32,2816]{1,0:T(8,128)(2,1)}, u32[]{:S(2)}) copy-start(bf16[32,2816]{1,0:T(8,128)(2,1)} %get-tuple-element.59) | copy-start | bytes 540676
  514.5 109.8 %slice-start.2 = ((s8[5767168]{0:T(1024)(128)(4,1)}), s8[1572864]{0:T(1024)(128)(4,1)S(1)}, s32[]{:S(2)}) async-start(s8[5767168]{0:T(1024)(128)(4,1)} %bitcast.135), calls=%async_computation.2 | async-start | bytes 3145728
  612.6 11.7 %slice-start.3 = ((s8[5767168]{0:T(1024)(128)(4,1)}), s8[4194304]{0:T(1024)(128)(4,1)S(1)}, s32[]{:S(2)}) async-start(s8[5767168]{0:T(1024)(128)(4,1)} %bitcast.135), calls=%async_computation.3 | async-start | bytes 8388608
  612.6 11.7 %copy-start = (bf16[2,2,2,2,2,32,2816]{6,5,4,3,2,1,0:T(8,128)(2,1)S(1)}, bf16[2,2,2,2,2,32,2816]{6,5,4,3,2,1,0:T(8,128)(2,1)}, u32[]{:S(2)}) copy-start(bf16[2,2,2,2,2,32,2816]{6,5,4,3,2,1,0:T(8,128)(2,1)} %get-tuple-element.63) | copy-start | bytes 17301508
  612.6 17.6 %slice-start = ((s8[5767168]{0:T(1024)(128)(4,1)}), s8[4194304]{0:T(1024)(128)(4,1)S(1)}, s32[]{:S(2)}) async-start(s8[5767168]{0:T(1024)(128)(4,1)} %bitcast.131), calls=%async_computation | async-start | bytes 8388608
  612.6 17.6 %slice-start.4 = ((s8[5767168]{0:T(1024)(128)(4,1)}), s8[4194304]{0:T(1024)(128)(4,1)S(1)}, s32[]{:S(2)}) async-start(s8[5767168]{0:T(1024)(128)(4,1)} %bitcast.138), calls=%async_computation.4 | async-start | bytes 8388608
  624.3 6.1 slice-start.1
  624.3 7.3 %slice-start.5 = ((s8[5767168]{0:T(1024)(128)(4,1)}), s8[1572864]{0:T(1024)(128)(4,1)S(1)}, s32[]{:S(2)}) async-start(s8[5767168]{0:T(1024)(128)(4,1)} %bitcast.138), calls=%async_computation.5 | async-start | bytes 3145728

commit v3 on v2

--- a/solution.py
+++ b/solution.py
@@ -13,9 +13,25 @@
 
 DIMS = {"x": 16, "y": 8, "b": 4, "a": 2, "c": 1}
 LEAD = "xyba"
-PARTS = {
-    2816: ((0, 1152, "xyab"), (1152, 2304, "yxab"), (2304, 2816, "abxy")),
-    1024: ((0, 384, "xyab"), (384, 768, "yxab"), (768, 1024, "abyx")),
+SUM_PARTS = {
+    "d1": ((0, 384, "xyab"), (384, 768, "yxab"), (768, 1024, "abxy")),
+    "g1": ((0, 1152, "xyab"), (1152, 2304, "yxab"), (2304, 2816, "abxy")),
+    "u1": ((0, 1024, "xyab"), (1024, 2048, "yxab"), (2048, 2816, "abyx")),
+    "d0": ((0, 512, "xyab"), (512, 1024, "yxab")),
+    "g0": ((0, 1024, "xyab"), (1024, 2048, "yxab"), (2048, 2816, "abxy")),
+    "u0": (
+        (0, 640, "xyab"),
+        (640, 1152, "yxab"),
+        (1152, 1536, "axyb"),
+        (1536, 1920, "ayxb"),
+        (1920, 2432, "abyx"),
+        (2432, 2816, "abxy"),
+    ),
+}
+NEW_PARTS = {
+    "d": ((0, 384, "xyab"), (384, 768, "yxab"), (768, 1024, "axyb")),
+    "g": ((0, 1024, "xyab"), (1024, 1920, "yxab"), (1920, 2432, "axyb"), (2432, 2816, "ayxb")),
+    "u": ((0, 896, "xyab"), (896, 1792, "yxab"), (1792, 2304, "axyb"), (2304, 2816, "ayxb")),
 }
 STEP = {32: 384, 88: 128}
 
@@ -45,16 +61,17 @@
     return [(at, min(step, hi - at)) for at in range(lo, hi, step)]
 
 
-def in_turn(steps, count):
-    return sorted(((k, i) for k in range(steps) for i in range(count)), key=lambda at: 1.5 * at[0] + at[1])
+def in_turn(chains):
+    turns = [(k, i, p) for k in range(5) for i, parts in enumerate(chains) for p in range(len(parts))]
+    return sorted(turns, key=lambda at: 1.5 * at[0] + at[1] * (0.3 if chains[at[1]][at[2]][2][0] == "a" else 1.0))
 
 
 class Scatter:
-    def __init__(self, grad, held, came, later, out, sems, local, first, own, peer):
+    def __init__(self, parts, grad, held, came, later, out, sems, local, first, own, peer):
         self.grad, self.held, self.came, self.later, self.out = grad, held, came, later, out
         self.own, self.peer = own, peer
         self.rows, self.cols = grad.shape[-2:]
-        self.parts = PARTS[self.cols]
+        self.parts = parts
         self.copies, n = {}, first
         for p, (lo, hi, order) in enumerate(self.parts):
             for half in range(2):
@@ -120,19 +137,16 @@
                 copy.wait_send()
 
 
-def copies_of(cols):
-    return len(PARTS[cols]) * 6
-
-
-def later_shapes(rows, cols):
-    return [[pltpu.VMEM((2,) * (3 - k) + (rows, hi - lo), BF16) for k in range(4)] for lo, hi, _ in PARTS[cols]]
+def later_shapes(parts, rows):
+    return [[pltpu.VMEM((2,) * (3 - k) + (rows, hi - lo), BF16) for k in range(4)] for lo, hi, _ in parts]
 
 
 class Gather:
-    def __init__(self, block, out, sems, local, first, own, peer):
+    def __init__(self, parts, block, out, sems, local, first, own, peer):
         rows, cols = block.shape
         every = slice(None)
-        self.parts = PARTS[cols]
+        self.parts = parts
+        self.kept = False
         self.keep = pltpu.make_async_copy(block, out.at[tuple(own[e] for e in LEAD) + (own["c"],)], local.at[first])
         self.copies, n = {}, first
         for p, (lo, hi, order) in enumerate(self.parts):
@@ -149,7 +163,8 @@
             self.keep.start()
 
     def send(self, p, k):
-        if k == 1 and p == 0:
+        if k == 1 and not self.kept:
+            self.kept = True
             self.keep.wait()
         if k:
             self.copies[k - 1, p].wait_recv()
@@ -162,11 +177,13 @@
             copy.wait_send()
 
 
-def host(name, body, steps, ins, outs, args, scratch=(), grads=(), blocks=(), collective_id=None, flops=0):
-    grads = [g.reshape((2,) * 5 + (g.shape[0] // 32, g.shape[1])) for g in grads]
+def host(name, body, steps, ins, outs, args, scratch=(), grads={}, blocks={}, collective_id=None, flops=0, ticks=1):
+    chains = [SUM_PARTS[name] for name in grads] + [NEW_PARTS[name] for name in blocks]
+    grads = [g.reshape((2,) * 5 + (g.shape[0] // 32, g.shape[1])) for g in grads.values()]
+    blocks = list(blocks.values())
     shapes = [g.shape[5:] for g in grads]
     counts = [len(ins), len(grads), len(blocks), len(outs), len(grads), len(blocks), len(scratch)]
-    total = sum(copies_of(s[1]) for s in shapes) + sum(5 * len(PARTS[b.shape[1]]) for b in blocks)
+    total = sum((6 if n < len(grads) else 5) * len(parts) for n, parts in enumerate(chains))
     anywhere, units_count = pl.BlockSpec(memory_space=pl.ANY), len(grads) + len(blocks)
 
     def kernel(*refs):
@@ -181,12 +198,12 @@
             own, peer = place()
             work, n = [], 0
             for i in range(len(grads)):
-                work.append(Scatter(grad_refs[i], held[i], came[i], later[i], sums[i], sems, local, n, own, peer))
+                work.append(Scatter(chains[i], grad_refs[i], held[i], came[i], later[i], sums[i], sems, local, n, own, peer))
                 n += work[-1].used
             for i in range(len(blocks)):
-                work.append(Gather(block_refs[i], gathered[i], sems, local, n, own, peer))
+                work.append(Gather(chains[len(grads) + i], block_refs[i], gathered[i], sems, local, n, own, peer))
                 n += work[-1].used
-            turns = in_turn(5, units_count)
+            turns = in_turn(chains)
 
             def begin():
                 greet(peer)
@@ -195,36 +212,41 @@
                         w.begin(half)
 
             def at(which):
-                for k, i in which:
-                    for p in range(len(work[i].parts)):
-                        work[i].send(p, k)
+                for k, i, p in which:
+                    work[i].send(p, k)
 
             def finish():
                 for w in work:
                     w.finish()
 
-            if steps == 1:
+            when, slots = {}, steps * ticks
+            for n, turn in enumerate(turns):
+                when.setdefault(1 + n * (slots - 1) // len(turns), []).append(turn)
+
+            def tick(j):
+                if j == 0:
+                    pl.when(step == 0)(begin)
+                for n in sorted(when):
+                    if n % ticks == j:
+                        pl.when(step == n // ticks)(functools.partial(at, when[n]))
+
+            if body is None:
                 begin()
                 at(turns)
                 finish()
-            else:
-                pl.when(step == 0)(begin)
-                when = {}
-                for n, turn in enumerate(turns):
-                    when.setdefault(1 + n * (steps - 1) // len(turns), []).append(turn)
-                for n, which in when.items():
-                    pl.when(step == n)(functools.partial(at, which))
+        else:
+            tick = lambda j: None
         if body is not None:
-            body(step, *mine, *results, *own_scratch)
-        if units_count and steps > 1:
-            pl.when(step == steps - 1)(finish)
+            body(step, tick, *mine, *results, *own_scratch)
+            if units_count:
+                pl.when(step == steps - 1)(finish)
 
     comm_scratch = []
     if units_count:
         comm_scratch = [
             [pltpu.VMEM((2, 2, 2, 2) + s, BF16) for s in shapes],
             [pltpu.VMEM((2, 2, 2, 2) + s, BF16) for s in shapes],
-            [later_shapes(*s) for s in shapes],
+            [later_shapes(parts, s[0]) for parts, s in zip(chains, shapes)],
             [pltpu.SemaphoreType.DMA((total,)), pltpu.SemaphoreType.DMA((total,))],
             pltpu.SemaphoreType.DMA((total,)),
         ]
@@ -348,7 +370,7 @@
     )(x, dy, wg, wu, wd)
 
 
-def back_body(step, dg1, du1, dy, h1, g0, u0, wg, wu, wd, dh1o, dg0o, du0o, wg1, wu1, wd0, sems):
+def back_body(step, tick, dg1, du1, dy, h1, g0, u0, wg, wu, wd, dh1o, dg0o, du0o, wg1, wu1, wd0, sems):
     copies = fetch([wg.at[1], wu.at[1], wd.at[0]], (wg1, wu1, wd0), sems)
 
     @pl.when(step == 0)
@@ -358,14 +380,18 @@
         for copy in copies:
             copy.wait()
 
+    tick(0)
     by_gate = dot(dg1[...], wg1[...], (1, 1)).astype(BF16)
+    tick(1)
     by_up = dot(du1[...], wu1[...], (1, 1)).astype(BF16)
     da = (by_gate + by_up).astype(F32)
     wide, r = scale_of(h1[...])
     inner = jnp.mean(da * wide, -1, keepdims=True)
     dh1o[...] = dy[...] + (da * r - wide * (r * r * r) * inner).astype(BF16)
     d = dh1o[...]
-    for at, size in CHUNKS:
+    for n, (at, size) in enumerate(CHUNKS):
+        if n % 3 == 0:
+            tick(2 + n // 3)
         cols = pl.ds(at, size)
         dp = dot(d, wd0[cols, :], (1, 1)).astype(BF16).astype(F32)
         s, ds = silu_parts(g0[:, cols])
@@ -387,6 +413,7 @@
         (dg1, du1, dy, h1, g0, u0, wg, wu, wd),
         [pltpu.VMEM(s, BF16) for s in ((d, ff), (d, ff), (ff, d))] + [pltpu.SemaphoreType.DMA((3,))],
         flops=6 * tokens * d * ff,
+        ticks=4,
         **beside,
     )
 
@@ -415,7 +442,8 @@
         outs.append((pl.BlockSpec((dim, tile), column(downs + n * tiles)), (dim, ff), BF16))
         args.append(w)
 
-    def work(step, *refs):
+    def work(step, tick, *refs):
+        tick(0)
         refs = list(refs)
         if p is not None:
             p_ref, d_ref = refs[:2]
@@ -448,7 +476,7 @@
     tokens, m = a.shape
     n = b.shape[1]
 
-    def work(step, a_ref, b_ref, o):
+    def work(step, tick, a_ref, b_ref, o):
         for at, size in HALVES:
             o[:, pl.ds(at, size)] = dot(a_ref[...], b_ref[:, pl.ds(at, size)], (0, 0)).astype(BF16)
 
@@ -462,21 +490,19 @@
     i = lax.axis_index(AXES)
 
     def update(layer, w, m, v, g):
-        rows = m.shape[1]
-        mine = lax.dynamic_slice_in_dim(w[layer], i * rows, rows, 0).astype(F32)
+        rows, cols = m.shape[1:]
+        mine = lax.dynamic_slice(w, (layer, i * rows, 0), (1, rows, cols))[0].astype(F32)
         return adamw(mine, m[layer], v[layer], g.astype(F32))
 
     a0, g0, u0, p0, h1, a1, p1, dg1, du1 = forth(x, dy, wg, wu, wd)
     dwd1 = outer(p1, dy)
-    (dwg1, dwu1), (sd1,), _ = outers(None, None, a1, [dg1, du1], grads=[dwd1], collective_id=0)
-    nd1 = update(1, wd, md, vd, sd1)
-    (dh1, dg0, du0), (sg1, su1), _ = back(dg1, du1, dy, h1, g0, u0, wg, wu, wd, grads=[dwg1, dwu1], collective_id=1)
-    ng1 = update(1, wg, mg, vg, sg1)
-    nu1 = update(1, wu, mu, vu, su1)
-    (dwd0, dwg0, dwu0), _, (fd1, fg1) = outers(p0, dh1, a0, [dg0, du0], blocks=[nd1[0], ng1[0]], collective_id=2)
-    _, (sd0, sg0, su0), (fu1,) = host("ends", None, 1, [], [], (), grads=[dwd0, dwg0, dwu0], blocks=[nu1[0]], collective_id=3)
+    (dwg1, dwu1), (sd1,), _ = outers(None, None, a1, [dg1, du1], grads={"d1": dwd1}, collective_id=0)
+    (dh1, dg0, du0), (sg1, su1), _ = back(dg1, du1, dy, h1, g0, u0, wg, wu, wd, grads={"g1": dwg1, "u1": dwu1}, collective_id=1)
+    nd1, ng1, nu1 = update(1, wd, md, vd, sd1), update(1, wg, mg, vg, sg1), update(1, wu, mu, vu, su1)
+    (dwd0, dwg0, dwu0), _, (fd1, fg1, fu1) = outers(p0, dh1, a0, [dg0, du0], blocks={"d": nd1[0], "g": ng1[0], "u": nu1[0]}, collective_id=2)
+    _, (sd0, sg0, su0), _ = host("ends", None, 1, [], [], (), grads={"d0": dwd0, "g0": dwg0, "u0": dwu0}, collective_id=3)
     nd0, ng0, nu0 = update(0, wd, md, vd, sd0), update(0, wg, mg, vg, sg0), update(0, wu, mu, vu, su0)
-    _, _, (fd0, fg0, fu0) = host("last", None, 1, [], [], (), blocks=[nd0[0], ng0[0], nu0[0]], collective_id=4)
+    _, _, (fd0, fg0, fu0) = host("last", None, 1, [], [], (), blocks={"d": nd0[0], "g": ng0[0], "u": nu0[0]}, collective_id=4)
     stacked = [jnp.stack(pair) for pair in ((fg0, fg1), (fu0, fu1), (fd0, fd1))]
     for which in (1, 2):
         stacked += [jnp.stack([a[which], b[which]]) for a, b in ((ng0, ng1), (nu0, nu1), (nd0, nd1))]

time: 637 us -> 589 us (0.925)
  local copies, waits for them, and re-layouts: 30.8 us -> 1.37 us
  Pallas kernels: 566 us -> 542 us
    slice x3 -> x0, local copies, waits for them, and re-layouts: 29.4 us -> none  [update(): mine = lax.dynamic_slice_in_dim(w[layer], i * rows, rows, 0).astype(F32)]
    pallas_call x6, Pallas kernels: 453 us -> 430 us  [host(): pl.pallas_call(kernel, name=name, grid=(steps,), in_specs=list(ins) + [an...]
where the time goes in v3:
time: 589 us; the launch traced here: 585 us
  Pallas kernels  542 us (92%)
  other arithmetic  40.2 us (7%)
    pallas_call x6, Pallas kernels, host(): pl.pallas_call(kernel, name=name, grid=(steps,), in_specs=list(ins) + [an...  430 us
    pallas_call x1, Pallas kernels, forth(): pl.pallas_call(forth_kernel, name='forth', grid=(tokens // TM,), in_specs...  112 us
    another operation x3, other arithmetic, body(): stacked = [jnp.stack(pair) for pair in ((fg0, fg1), (fu0, fu1), (fd0, fd1))]  22.6 us
    another operation x11, other arithmetic, body(): jnp.stack([a[which], b[which]])  17.6 us

profile of v3, /device:TPU:0, one launch (start us, length us, event | category | flops | bytes accessed | tf_op | source)
XLA Modules:
  0.0 584.7 jit_solution(13504395892276945747)
XLA Ops:
  0.6 112.5 %forth.1 = (bf16[2048,1024]{1,0:T(8,128)(2,1)}, f32[2048,2816]{1,0:T(8,128)}, f32[2048,2816]{1,0:T(8,128)}, bf16[2048,2816]{1,0:T(8,128)(2,1)}, bf16[2048,1024]{...) custom-call(bf16[2048,1024]{1,0:T(8,128)(2,1)} %bitcast.143, ...), custom_call_target="tpu_custom_call" | custom-call | flops 70866960384 | bytes 188743680 | tf_op jit(solution)/shard_map/forth/pallas_call | solution.py:360
  113.1 18.2 %outer.1 = bf16[2816,1024]{1,0:T(8,128)(2,1)} custom-call(bf16[2048,2816]{1,0:T(8,128)(2,1)} %get-tuple-element.45.refs_0_, bf16[2048,1024]{1,0:T(8,128)(2,1)} %bitcast.145), custom_call_target="tpu_custom_call" | custom-call | flops 12811159552 | bytes 62914560 | tf_op jit(solution)/shard_map/outer/pallas_call | solution.py:255
  131.3 55.8 %outers.2 = (bf16[1024,2816]{1,0:T(8,128)(2,1)}, bf16[1024,2816]{1,0:T(8,128)(2,1)}, bf16[88,1024]{1,0:T(8,128)(2,1)}) custom-call(bf16[2048,1024]{1,0:T(8,128)(2,1)} %get-tuple-element.44.refs_0_, bf16[2048,2816]{1,0:T(8,128)(2,1)} %get-tuple-element.39.refs_1_.refs_0_, bf16[2048,2816]{1,0:T(8,128)(2,1)} %get-tuple-element.40.refs_2_.refs_1_, ...), custom_call_target="tpu_custom_call" | custom-call | flops 24622319616 | bytes 62914560 | tf_op jit(solution)/shard_map/outers/pallas_call | solution.py:255
  187.1 85.5 %back.1 = (bf16[2048,1024]{1,0:T(8,128)(2,1)}, bf16[2048,2816]{1,0:T(8,128)(2,1)}, bf16[2048,2816]{1,0:T(8,128)(2,1)}, bf16[32,2816]{1,0:T(8,128)(2,1)}, bf16[32,2816]{1,0:T(8,128)(2,1)}) custom-call(bf16[2048,2816]{1,0:T(8,128)(2,1)} %get-tuple-element.39.refs_1_.refs_0_, bf16[2048,2816]{1,0:T(8,128)(2,1)} %get-tuple-element.40.refs_2_.refs_1_, ...), custom_call_target="tpu_custom_call" | custom-call | flops 36433481728 | bytes 62914560 | tf_op jit(solution)/shard_map/back/pallas_call | solution.py:255
  272.6 2.7 fusion.38
  275.3 2.1 fusion.41
  277.4 101.2 %outers.3 = (bf16[2816,1024]{1,0:T(8,128)(2,1)}, bf16[1024,2816]{1,0:T(8,128)(2,1)}, bf16[1024,2816]{1,0:T(8,128)(2,1)}, bf16[2,2,2,2,2,88,1024]{6,5,4,3,2,1,0:T...) custom-call(bf16[2048,2816]{1,0:T(8,128)(2,1)} %get-tuple-element.38.refs_0_, ...), custom_call_target="tpu_custom_call" | custom-call | flops 36433481728 | bytes 62914560 | tf_op jit(solution)/shard_map/outers/pallas_call | solution.py:255
  378.7 81.4 %ends.1 = (bf16[88,1024]{1,0:T(8,128)(2,1)}, bf16[32,2816]{1,0:T(8,128)(2,1)}, bf16[32,2816]{1,0:T(8,128)(2,1)}) custom-call(bf16[2,2,2,2,2,88,1024]{6,5,4,3,2,1,0:T(8,128)(2,1)} %bitcast.128, bf16[2,2,2,2,2,32,2816]{6,5,4,3,2,1,0:T(8,128)(2,1)} %bitcast.129, bf16[2,2,2,2,2,32,2816]{6,5,4,3,2,1,0:T(8,128)(2,1)} %bitcast.130), custom_call_target="tpu_custom_call" | custom-call | flops 1000000000 | bytes 62914560 | tf_op jit(solution)/shard_map/ends/pallas_call | solution.py:255
  460.1 2.1 fusion.40
  462.2 1.9 pad_maximum_fusion.8
  464.1 2.1 fusion.36
  466.2 0.9 pad_maximum_fusion.7
  467.1 2.1 fusion.37
  469.2 0.9 pad_maximum_fusion.6
  470.1 0.9 pad_maximum_fusion.5
  471.0 0.9 pad_maximum_fusion.4
  471.9 0.9 pad_maximum_fusion.3
  472.8 87.8 %last.1 = (bf16[2,2,2,2,2,88,1024]{6,5,4,3,2,1,0:T(8,128)(2,1)}, bf16[2,2,2,2,2,32,2816]{6,5,4,3,2,1,0:T(8,128)(2,1)}, bf16[2,2,2,2,2,32,2816]{6,5,4,3,2,1,0:T(8,128)(2,1)}) custom-call(bf16[88,1024]{1,0:T(8,128)(2,1)} %get-tuple-element.68.refs_0_, bf16[32,2816]{1,0:T(8,128)(2,1)} %get-tuple-element.80.refs_1_, bf16[32,2816]{1,0:T(8,128)(2,1)} %get-tuple-element.74.refs_2_), custom_call_target="tpu_custom_call" | custom-call | flops 1000000000 | bytes 62914560 | tf_op jit(solution)/shard_map/last/pallas_call | solution.py:255
  560.7 0.0 slice-start.3
  560.7 11.7 %pad_maximum_fusion.2 = bf16[2,2816,1024]{2,1,0:T(8,128)(2,1)} fusion(bf16[1,2816,1024]{2,1,0:T(8,128)(2,1)} %bitcast.137, bf16[1,2816,1024]{2,1,0:T(8,128)(2,1)} %bitcast.142), kind=kLoop, calls=%fused_computation.2 | loop fusion | flops 5767168 | bytes 23068672 | tf_op jit(solution)/shard_map/stack | solution.py:506
  572.4 5.9 %pad_maximum_fusion.1 = bf16[2,1024,2816]{2,1,0:T(8,128)(2,1)} fusion(bf16[1,1024,2816]{2,1,0:T(8,128)(2,1)S(1)} %bitcast.136, bf16[1,1024,2816]{2,1,0:T(8,128)(2,1)S(1)} %bitcast.141), kind=kLoop, calls=%fused_computation.1 | loop fusion | flops 5767168 | bytes 23068672 | tf_op jit(solution)/shard_map/stack | solution.py:506
  578.3 0.2 slice-done.1
  578.5 1.1 slice-done.5
  579.7 5.0 pad_maximum_fusion
  (16 shorter events, 0.0 us)
Async XLA Ops:
  187.1 88.2 %copy-start.1 = (bf16[88,1024]{1,0:T(8,128)(2,1)S(1)}, bf16[88,1024]{1,0:T(8,128)(2,1)}, u32[]{:S(2)}) copy-start(bf16[88,1024]{1,0:T(8,128)(2,1)} %get-tuple-element.52) | copy-start | bytes 540676
  472.8 99.6 %slice-start.2 = ((s8[5767168]{0:T(1024)(128)(4,1)}), s8[1572864]{0:T(1024)(128)(4,1)S(1)}, s32[]{:S(2)}) async-start(s8[5767168]{0:T(1024)(128)(4,1)} %bitcast.134), calls=%async_computation.2 | async-start | bytes 3145728
  560.7 11.7 %slice-start.3 = ((s8[5767168]{0:T(1024)(128)(4,1)}), s8[4194304]{0:T(1024)(128)(4,1)S(1)}, s32[]{:S(2)}) async-start(s8[5767168]{0:T(1024)(128)(4,1)} %bitcast.134), calls=%async_computation.3 | async-start | bytes 8388608
  560.7 11.7 %copy-start = (bf16[2,2,2,2,2,32,2816]{6,5,4,3,2,1,0:T(8,128)(2,1)S(1)}, bf16[2,2,2,2,2,32,2816]{6,5,4,3,2,1,0:T(8,128)(2,1)}, u32[]{:S(2)}) copy-start(bf16[2,2,2,2,2,32,2816]{6,5,4,3,2,1,0:T(8,128)(2,1)} %get-tuple-element.63) | copy-start | bytes 17301508
  560.7 17.6 %slice-start = ((s8[5767168]{0:T(1024)(128)(4,1)}), s8[4194304]{0:T(1024)(128)(4,1)S(1)}, s32[]{:S(2)}) async-start(s8[5767168]{0:T(1024)(128)(4,1)} %bitcast.131), calls=%async_computation | async-start | bytes 8388608
  560.7 17.6 %slice-start.4 = ((s8[5767168]{0:T(1024)(128)(4,1)}), s8[4194304]{0:T(1024)(128)(4,1)S(1)}, s32[]{:S(2)}) async-start(s8[5767168]{0:T(1024)(128)(4,1)} %bitcast.138), calls=%async_computation.4 | async-start | bytes 8388608
  572.4 6.1 %slice-start.1 = ((s8[5767168]{0:T(1024)(128)(4,1)}), s8[1572864]{0:T(1024)(128)(4,1)S(1)}, s32[]{:S(2)}) async-start(s8[5767168]{0:T(1024)(128)(4,1)} %bitcast.131), calls=%async_computation.1 | async-start | bytes 3145728
  572.4 7.3 %slice-start.5 = ((s8[5767168]{0:T(1024)(128)(4,1)}), s8[1572864]{0:T(1024)(128)(4,1)S(1)}, s32[]{:S(2)}) async-start(s8[5767168]{0:T(1024)(128)(4,1)} %bitcast.138), calls=%async_computation.5 | async-start | bytes 3145728
